TPU v7x, 32 devices: a whole 2x2x4 slice. The times are simulated.
32 devices in a mesh: seq: 8 (over z, y), head: 4 (over x, core).
Axes of the slice: x: 2, y: 2, z: 4, core: 2. Of those that a mesh axis runs over, the one named last changes fastest.
Arguments:
- queries: bfloat16 [6144, 4096], P(('seq', 'head')), may hold values from -6 to 6
- key_rows: bfloat16 [6144, 4096], P(('seq', 'head')), may hold values from -6 to 6
- values: bfloat16 [6144, 4096], P(('seq', 'head')), may hold values from -6 to 6
- doc_ids: int32 [6144], replicated, may hold values from 0 to 15, as said below
- image_flags: int32 [6144], replicated, may hold values from 0 to 1, as said below
- labels: int32 [6144], P(('seq', 'head')), may hold values from -1 to 31999, as said below
- token_loss: float32 [6144], P(('seq', 'head')), may hold values from 0.05 to 8
Outputs:
- attended: bfloat16 [6144, 4096], P(('seq', 'head'))
- doc_count: float32 [16], replicated
- doc_loss: float32 [16], replicated
Inputs may be any that keep to these rules, and one draw needn't show every extreme that they name: `doc_ids`: document numbers never fall along the sequence and rise by one from one document to the next; every document holds at least 64 and at most 704 tokens, and some document holds exactly 704. `image_flags`: the 1s form spans of exactly 576 consecutive tokens, at most one span a document, each inside one document and never at its first token. `labels`: every image token has -1, and some document has -1 on all of its tokens.
All inputs are finite; a program needn't handle non-finite values.
Results may differ from a plain program's by a relative error of at most 0.0034.
Values may be sent and summed in bfloat16 or wider, within the bound.
No kernel may reach another device: no remote copies, remote signals or barrier semaphores. Data moves between devices by JAX's collectives and lax.ppermute only.
A program may use at most 128 MiB of HBM per device.

v0:
```python
import jax
import jax.numpy as jnp
from jax import lax
from jax.sharding import PartitionSpec as P

HEAD_DIM = 128
TOK_DEV = 768
DOC_MEAN = 384
DOC_MOST = 704
IMG_LEN = 576


def shifted(block, axis, distance):
    devices = range(lax.axis_size(axis))
    route = [(i - distance, i) for i in devices if i - distance in devices]
    return lax.ppermute(block, axis, route)


def cut_rows(reach):
    return min(TOK_DEV, -(-reach // 128) * 128)


def allowed_pairs(query_docs, query_flags, query_places, key_docs, key_flags, key_places):
    same = query_docs[:, None] == key_docs[None, :]
    earlier = key_places[None, :] <= query_places[:, None]
    image = (query_flags[:, None] == 1) & (key_flags[None, :] == 1)
    return same & (earlier | image)


def attend(query_part, key_window, value_window, allowed):
    outputs = []
    scale = HEAD_DIM ** (-0.5)
    for head_index in range(query_part.shape[1] // HEAD_DIM):
        lower = head_index * HEAD_DIM
        query_head = query_part[:, lower : lower + HEAD_DIM]
        key_head = key_window[:, lower : lower + HEAD_DIM]
        value_head = value_window[:, lower : lower + HEAD_DIM]
        scores = (
            lax.dot_general(
                query_head, key_head, (((1,), (1,)), ((), ())), preferred_element_type=jnp.float32
            )
            * scale
        )
        scores = jnp.where(allowed, scores, -jnp.inf)
        row_max = jnp.max(scores, axis=1, keepdims=True)
        weights = jnp.exp(scores - row_max)
        total = jnp.sum(weights, axis=1, keepdims=True)
        mixed = (
            jnp.dot(weights.astype(jnp.bfloat16), value_head, preferred_element_type=jnp.float32)
            / total
        )
        outputs.append(mixed.astype(jnp.bfloat16))
    return jnp.concatenate(outputs, axis=1)


def per_device(queries, key_rows, values, doc_ids, image_flags, labels, token_loss):
    query_local, key_local, value_local = (
        lax.all_to_all(queries, "head", split_axis=1, concat_axis=0, tiled=True),
        lax.all_to_all(key_rows, "head", split_axis=1, concat_axis=0, tiled=True),
        lax.all_to_all(values, "head", split_axis=1, concat_axis=0, tiled=True),
    )
    reach_back = (DOC_MOST + TOK_DEV - 2) // TOK_DEV
    reach_front = (IMG_LEN + TOK_DEV - 2) // TOK_DEV
    behind = [shifted((key_local, value_local), "seq", 1)]
    ahead = [
        shifted(
            (
                key_local[: cut_rows(IMG_LEN - 1 - (1 - 1) * TOK_DEV)],
                value_local[: cut_rows(IMG_LEN - 1 - (1 - 1) * TOK_DEV)],
            ),
            "seq",
            -1,
        )
    ]
    key_window = jnp.concatenate(
        [pair[0] for pair in behind] + [key_local] + [pair[0] for pair in ahead], axis=0
    )
    value_window = jnp.concatenate(
        [pair[1] for pair in behind] + [value_local] + [pair[1] for pair in ahead], axis=0
    )
    back_total = sum((pair[0].shape[0] for pair in behind))
    window_rows = key_window.shape[0]
    block_start = lax.axis_index("seq") * TOK_DEV
    pad_front = reach_back * TOK_DEV
    pad_back = reach_front * TOK_DEV
    padded_docs = jnp.pad(doc_ids, (pad_front, pad_back), constant_values=-1)
    padded_flags = jnp.pad(image_flags, (pad_front, pad_back))
    key_docs = lax.dynamic_slice_in_dim(
        padded_docs, block_start + pad_front - back_total, window_rows
    )
    key_flags = lax.dynamic_slice_in_dim(
        padded_flags, block_start + pad_front - back_total, window_rows
    )
    query_docs = lax.dynamic_slice_in_dim(doc_ids, block_start, TOK_DEV)
    query_flags = lax.dynamic_slice_in_dim(image_flags, block_start, TOK_DEV)
    query_places = block_start + jnp.arange(TOK_DEV, dtype=jnp.int32)
    key_places = block_start - back_total + jnp.arange(window_rows, dtype=jnp.int32)
    allowed = allowed_pairs(query_docs, query_flags, query_places, key_docs, key_flags, key_places)
    attended = attend(query_local, key_window, value_window, allowed)
    output = lax.all_to_all(attended, "head", split_axis=0, concat_axis=1, tiled=True)
    local_rows = labels.shape[0]
    row_start = (
        lax.axis_index("seq") * lax.axis_size("head") + lax.axis_index("head")
    ) * local_rows
    local_docs = lax.dynamic_slice_in_dim(doc_ids, row_start, local_rows)
    documents = doc_ids.shape[0] // DOC_MEAN
    member = (local_docs[:, None] == jnp.arange(documents, dtype=jnp.int32)[None, :]) & (
        labels[:, None] >= 0
    )
    counts = jnp.sum(member.astype(jnp.float32), axis=0)
    sums = jnp.sum(jnp.where(member, token_loss[:, None], jnp.float32(0.0)), axis=0)
    counts, sums = lax.psum((counts, sums), ("seq", "head"))
    return (output, counts, sums / jnp.maximum(counts, jnp.float32(1.0)))


def solution(mesh):
    in_specs = (
        P(("seq", "head"), None),
        P(("seq", "head"), None),
        P(("seq", "head"), None),
        P(),
        P(),
        P(("seq", "head")),
        P(("seq", "head")),
    )
    out_specs = (P(("seq", "head"), None), P(), P())
    return jax.shard_map(
        per_device, mesh=mesh, in_specs=in_specs, out_specs=out_specs, check_vma=False
    )
```

profile of v0, /device:TPU:0, one launch (start us, length us, event | category | flops | bytes accessed | tf_op | source)
XLA Modules:
  0.0 272.2 jit_solution(8038829767457793462)
XLA Ops:
  3.5 4.2 %all-to-all-start = ((bf16[192,4,1024]{2,0,1:T(8,128)(2,1)}), bf16[192,4,1024]{2,0,1:T(8,128)(2,1)S(1)}, u32[]{:S(2)}, u32[]{:S(2)}) async-start(bf16[192,4,1024]{2,0,1:T(8,128)(2,1)} %bitcast.40), calls=%async_computation | async-start | bytes 3145728 | tf_op jit(solution)/shard_map/all_to_all | solution.py:59
  9.0 18.7 %all-to-all-done = bf16[192,4,1024]{2,0,1:T(8,128)(2,1)S(1)} async-done(((bf16[192,4,1024]{2,0,1:T(8,128)(2,1)}), bf16[192,4,1024]{2,0,1:T(8,128)(2,1)S(1)}, u32[]{:S(2)}, u32[]{:S(2)}) %all-to-all-start) | async-done | bytes 1572896 | tf_op jit(solution)/shard_map/all_to_all | solution.py:59
  27.7 3.6 %all-to-all-start.2 = ((bf16[192,4,1024]{2,0,1:T(8,128)(2,1)}), bf16[192,4,1024]{2,0,1:T(8,128)(2,1)S(1)}, u32[]{:S(2)}, u32[]{:S(2)}) async-start(bf16[192,4,1024]{2,0,1:T(8,128)(2,1)} %bitcast.53), calls=%async_computation.2 | async-start | bytes 3145728 | tf_op jit(solution)/shard_map/all_to_all | solution.py:60
  31.3 5.4 %collective-permute-start = (bf16[768,1024]{1,0:T(8,128)(2,1)S(1)}, bf16[768,1024]{1,0:T(8,128)(2,1)}, u32[]{:S(2)}, u32[]{:S(2)}) collective-permute-start(bf16[768,1024]{1,0:T(8,128)(2,1)S(1)} %bitcast.44), channel_id=1, source_target_pairs={{0,4},{4,8},{8,12},{12,16},{16,20},{20,24},{24,28},{1,5},{5,9},{9,... | collective-permute-start | bytes 4718600 | tf_op jit(solution)/shard_map/ppermute | solution.py:16
  41.9 9.4 %all-to-all-done.2 = bf16[192,4,1024]{2,0,1:T(8,128)(2,1)S(1)} async-done(((bf16[192,4,1024]{2,0,1:T(8,128)(2,1)}), bf16[192,4,1024]{2,0,1:T(8,128)(2,1)S(1)}, u32[]{:S(2)}, u32[]{:S(2)}) %all-to-all-start.2) | async-done | bytes 1572896 | tf_op jit(solution)/shard_map/all_to_all | solution.py:60
  51.3 4.3 %all-to-all-start.1 = ((bf16[192,4,1024]{2,0,1:T(8,128)(2,1)}), bf16[192,4,1024]{2,0,1:T(8,128)(2,1)}, u32[]{:S(2)}, u32[]{:S(2)}) async-start(bf16[192,4,1024]{2,0,1:T(8,128)(2,1)} %bitcast.51), calls=%async_computation.1 | async-start | bytes 3145728 | tf_op jit(solution)/shard_map/all_to_all | solution.py:58
  57.2 5.3 %collective-permute-start.2 = (bf16[768,1024]{1,0:T(8,128)(2,1)S(1)}, bf16[768,1024]{1,0:T(8,128)(2,1)}, u32[]{:S(2)}, u32[]{:S(2)}) collective-permute-start(bf16[768,1024]{1,0:T(8,128)(2,1)S(1)} %bitcast.42), channel_id=1, source_target_pairs={{0,4},{4,8},{8,12},{12,16},{16,20},{20,24},{24,28},{1,5},{5,9},{9,... | collective-permute-start | bytes 4718600 | tf_op jit(solution)/shard_map/ppermute | solution.py:16
  63.9 7.9 %collective-permute-done.1 = bf16[640,1024]{1,0:T(8,128)(2,1)} collective-permute-done((bf16[640,1024]{1,0:T(8,128)(2,1)}, bf16[640,1024]{1,0:T(8,128)(2,1)}, u32[]{:S(2)}, u32[]{:S(2)}) %collective-permute-start.1) | collective-permute-done | bytes 1310752 | tf_op jit(solution)/shard_map/ppermute | solution.py:16
  71.8 54.7 %collective-permute-done = bf16[768,1024]{1,0:T(8,128)(2,1)} collective-permute-done((bf16[768,1024]{1,0:T(8,128)(2,1)S(1)}, bf16[768,1024]{1,0:T(8,128)(2,1)}, u32[]{:S(2)}, u32[]{:S(2)}) %collective-permute-start) | collective-permute-done | bytes 1572896 | tf_op jit(solution)/shard_map/ppermute | solution.py:16
  126.5 3.6 %pad_maximum_fusion = bf16[2176,1024]{1,0:T(8,128)(2,1)} fusion(bf16[640,1024]{1,0:T(8,128)(2,1)} %collective-permute-done.1, bf16[768,1024]{1,0:T(8,128)(2,1)S(1)} %bitcast.46, bf16[768,1024]{1,0:T(8,128)(2,1)} %collective-permute-done), kind=kLoop, calls=%fused_computation.33 | loop fusion | flops 13369344 | bytes 8912896 | tf_op jit(solution)/shard_map/concatenate | solution.py:75
  130.1 4.2 %fusion.138 = (f32[768]{0:T(1024)S(1)}, f32[768,2176]{0,1:T(8,128)S(1)}) fusion(bf16[768,1024]{1,0:T(8,128)(2,1)} %bitcast.4, bf16[2176,1024]{1,0:T(8,128)(2,1)} %pad_maximum_fusion, pred[2176]{0:T(1024)(128)(4,1)S(1)} %fusion.137, pred[768]{0:T(1024)(128)(4,1)S(1)} %dynamic-slice_compare_fusion, s32[768]{0:T(1024)S(1)} %iota_add_fusion.1, ...), kind=kOutput, calls=%fused_computation.114 | convolution fusion | flops 441187584 | bytes 7467904 | tf_op jit(solution)/shard_map/dot_general | solution.py:39
  134.4 6.3 %fusion.139 = (f32[768]{0:T(1024)S(1)}, f32[768,2176]{0,1:T(8,128)}) fusion(bf16[768,1024]{1,0:T(8,128)(2,1)} %bitcast.4, bf16[2176,1024]{1,0:T(8,128)(2,1)S(1)} %copy-done.1, pred[2176]{0:T(1024)(128)(4,1)S(1)} %fusion.137, pred[768]{0:T(1024)(128)(4,1)S(1)} %dynamic-slice_compare_fusion, s32[768]{0:T(1024)S(1)} %iota_add_fusion.1, ...), kind=kOutput, calls=%fused_computation.115 | convolution fusion | flops 441187584 | bytes 7478272 | tf_op jit(solution)/shard_map/dot_general | solution.py:39
  140.7 5.9 %fusion.140 = (f32[768]{0:T(1024)S(1)}, f32[768,2176]{0,1:T(8,128)}) fusion(bf16[768,1024]{1,0:T(8,128)(2,1)} %bitcast.4, bf16[2176,1024]{1,0:T(8,128)(2,1)S(1)} %copy-done.1, pred[2176]{0:T(1024)(128)(4,1)S(1)} %fusion.137, pred[768]{0:T(1024)(128)(4,1)S(1)} %dynamic-slice_compare_fusion, s32[768]{0:T(1024)S(1)} %iota_add_fusion.1, ...), kind=kOutput, calls=%fused_computation.116 | convolution fusion | flops 441187584 | bytes 7478272 | tf_op jit(solution)/shard_map/dot_general | solution.py:39
  146.6 6.0 %fusion.141 = (f32[768]{0:T(1024)S(1)}, f32[768,2176]{0,1:T(8,128)}) fusion(bf16[768,1024]{1,0:T(8,128)(2,1)} %bitcast.4, bf16[2176,1024]{1,0:T(8,128)(2,1)S(1)} %copy-done.1, pred[2176]{0:T(1024)(128)(4,1)S(1)} %fusion.137, pred[768]{0:T(1024)(128)(4,1)S(1)} %dynamic-slice_compare_fusion, s32[768]{0:T(1024)S(1)} %iota_add_fusion.1, ...), kind=kOutput, calls=%fused_computation.117 | convolution fusion | flops 441187584 | bytes 7478272 | tf_op jit(solution)/shard_map/dot_general | solution.py:39
  152.5 3.6 %fusion.142 = (f32[768]{0:T(1024)S(1)}, f32[768,2176]{0,1:T(8,128)S(1)}) fusion(bf16[768,1024]{1,0:T(8,128)(2,1)} %bitcast.4, bf16[2176,1024]{1,0:T(8,128)(2,1)S(1)} %copy-done.1, pred[2176]{0:T(1024)(128)(4,1)S(1)} %fusion.137, pred[768]{0:T(1024)(128)(4,1)S(1)} %dynamic-slice_compare_fusion, s32[768]{0:T(1024)S(1)} %iota_add_fusion.1, ...), kind=kOutput, calls=%fused_computation.118 | convolution fusion | flops 441187584 | bytes 7478272 | tf_op jit(solution)/shard_map/dot_general | solution.py:39
  156.2 3.6 %fusion.143 = (f32[768]{0:T(1024)S(1)}, f32[768,2176]{0,1:T(8,128)S(1)}) fusion(bf16[768,1024]{1,0:T(8,128)(2,1)} %bitcast.4, bf16[2176,1024]{1,0:T(8,128)(2,1)S(1)} %copy-done.1, pred[2176]{0:T(1024)(128)(4,1)S(1)} %fusion.137, pred[768]{0:T(1024)(128)(4,1)S(1)} %dynamic-slice_compare_fusion, s32[768]{0:T(1024)S(1)} %iota_add_fusion.1, ...), kind=kOutput, calls=%fused_computation.119 | convolution fusion | flops 441187584 | bytes 7478272 | tf_op jit(solution)/shard_map/dot_general | solution.py:39
  160.8 3.6 %fusion.144 = (f32[768]{0:T(1024)S(1)}, f32[768,2176]{0,1:T(8,128)S(1)}) fusion(bf16[768,1024]{1,0:T(8,128)(2,1)} %bitcast.4, bf16[2176,1024]{1,0:T(8,128)(2,1)S(1)} %copy-done.1, pred[2176]{0:T(1024)(128)(4,1)S(1)} %fusion.137, pred[768]{0:T(1024)(128)(4,1)S(1)} %dynamic-slice_compare_fusion, s32[768]{0:T(1024)S(1)} %iota_add_fusion.1, ...), kind=kOutput, calls=%fused_computation.120 | convolution fusion | flops 441187584 | bytes 7478272 | tf_op jit(solution)/shard_map/dot_general | solution.py:39
  164.5 3.9 %fusion.145 = (f32[768]{0:T(1024)S(1)}, f32[768,2176]{0,1:T(8,128)S(1)}) fusion(bf16[768,1024]{1,0:T(8,128)(2,1)} %bitcast.4, bf16[2176,1024]{1,0:T(8,128)(2,1)S(1)} %copy-done.1, pred[2176]{0:T(1024)(128)(4,1)S(1)} %fusion.137, pred[768]{0:T(1024)(128)(4,1)S(1)} %dynamic-slice_compare_fusion, s32[768]{0:T(1024)S(1)} %iota_add_fusion.1, ...), kind=kOutput, calls=%fused_computation.121 | convolution fusion | flops 441187584 | bytes 7478272 | tf_op jit(solution)/shard_map/dot_general | solution.py:39
  168.4 3.9 %pad_maximum_fusion.1 = bf16[2176,1024]{1,0:T(8,128)(2,1)} fusion(bf16[640,1024]{1,0:T(8,128)(2,1)} %collective-permute-done.3, bf16[768,1024]{1,0:T(8,128)(2,1)S(1)} %bitcast.43, bf16[768,1024]{1,0:T(8,128)(2,1)} %collective-permute-done.2), kind=kLoop, calls=%fused_computation.34 | loop fusion | flops 13369344 | bytes 8912896 | tf_op jit(solution)/shard_map/concatenate | solution.py:78
  172.2 4.3 %fusion.46 = bf16[768,1024]{0,1:T(8,128)(2,1)S(1)} fusion(f32[768,2176]{0,1:T(8,128)} %copy-done, f32[768]{0:T(1024)S(1)} %get-tuple-element.7, bf16[2176,1024]{1,0:T(8,128)(2,1)} %pad_maximum_fusion.1, f32[768]{0:T(1024)S(1)} %fusion), kind=kOutput, calls=%fused_computation.56 | convolution fusion | flops 431357952 | bytes 7444480 | tf_op jit(solution)/shard_map/dot_general | solution.py:49
  179.8 4.0 %fusion.4 = f32[768]{0:T(1024)S(1)} fusion(f32[768,2176]{0,1:T(8,128)} %get-tuple-element.12, f32[768]{0:T(1024)S(1)} %get-tuple-element.11), kind=kLoop, calls=%fused_computation.21 | loop fusion | flops 3341568 | bytes 6690816 | tf_op jit(solution)/shard_map/reduce_sum | solution.py:47
  183.8 4.3 %fusion.64 = bf16[768,1024]{0,1:T(8,128)(2,1)S(1)} fusion(bf16[768,1024]{0,1:T(8,128)(2,1)S(1)} %fusion.55, f32[768,2176]{0,1:T(8,128)} %get-tuple-element.12, f32[768]{0:T(1024)S(1)} %get-tuple-element.11, bf16[2176,1024]{1,0:T(8,128)(2,1)} %pad_maximum_fusion.1, f32[768]{0:T(1024)S(1)} %fusion.4), kind=kOutput, calls=%fused_computation.62 | convolution fusion | flops 431357952 | bytes 7446528 | tf_op jit(solution)/shard_map/dot_general | solution.py:49
  206.2 3.6 %all-to-all-start.3 = ((bf16[4,192,1024]{2,1,0:T(8,128)(2,1)}), bf16[4,192,1024]{2,1,0:T(8,128)(2,1)S(1)}, u32[]{:S(2)}, u32[]{:S(2)}) async-start(bf16[4,192,1024]{2,1,0:T(8,128)(2,1)} %bitcast.17), calls=%async_computation.3 | async-start | bytes 3145728 | tf_op jit(solution)/shard_map/all_to_all | solution.py:100
  210.0 60.4 %all-reduce.2 = (f32[16]{0:T(128)S(1)}, f32[16]{0:T(128)S(1)}) all-reduce(f32[16]{0:T(128)S(1)} %get-tuple-element.4, f32[16]{0:T(128)S(1)} %get-tuple-element.3), channel_id=1, replica_groups=mesh['seq'=8,'head'=4] {'seq','head'}, use_global_device_ids=true, to_apply=%region_17.18 | all-reduce | flops 32 | bytes 256 | tf_op jit(solution)/shard_map/psum | solution.py:112
  (62 shorter events, 36.3 us)
Async XLA Ops:
  0.6 7.1 %copy-start.2 = (bf16[192,4096]{1,0:T(8,128)(2,1)S(1)}, bf16[192,4096]{1,0:T(8,128)(2,1)}, u32[]{:S(2)}) copy-start(bf16[192,4096]{1,0:T(8,128)(2,1)} %param.9) | copy-start | bytes 4718596
  3.5 24.3 %all-to-all-start = ((bf16[192,4,1024]{2,0,1:T(8,128)(2,1)}), bf16[192,4,1024]{2,0,1:T(8,128)(2,1)S(1)}, u32[]{:S(2)}, u32[]{:S(2)}) async-start(bf16[192,4,1024]{2,0,1:T(8,128)(2,1)} %bitcast.40), calls=%async_computation | async-start | bytes 3145728 | tf_op jit(solution)/shard_map/all_to_all | solution.py:59
  27.7 23.6 %all-to-all-start.2 = ((bf16[192,4,1024]{2,0,1:T(8,128)(2,1)}), bf16[192,4,1024]{2,0,1:T(8,128)(2,1)S(1)}, u32[]{:S(2)}, u32[]{:S(2)}) async-start(bf16[192,4,1024]{2,0,1:T(8,128)(2,1)} %bitcast.53), calls=%async_computation.2 | async-start | bytes 3145728 | tf_op jit(solution)/shard_map/all_to_all | solution.py:60
  31.3 24.4 %copy-start.3 = (s32[6144]{0:T(1024)S(1)}, s32[6144]{0:T(1024)}, u32[]{:S(2)}) copy-start(s32[6144]{0:T(1024)} %param.10) | copy-start | bytes 73732
  31.3 24.5 %copy-start.4 = (s32[6144]{0:T(1024)S(1)}, s32[6144]{0:T(1024)}, u32[]{:S(2)}) copy-start(s32[6144]{0:T(1024)} %param.11) | copy-start | bytes 73732
  31.3 95.2 %collective-permute-start = (bf16[768,1024]{1,0:T(8,128)(2,1)S(1)}, bf16[768,1024]{1,0:T(8,128)(2,1)}, u32[]{:S(2)}, u32[]{:S(2)}) collective-permute-start(bf16[768,1024]{1,0:T(8,128)(2,1)S(1)} %bitcast.44), channel_id=1, source_target_pairs={{0,4},{4,8},{8,12},{12,16},{16,20},{20,24},{24,28},{1,5},{5,9},{9,... | collective-permute-start | bytes 4718600 | tf_op jit(solution)/shard_map/ppermute | solution.py:16
  37.9 33.8 %collective-permute-start.1 = (bf16[640,1024]{1,0:T(8,128)(2,1)}, bf16[640,1024]{1,0:T(8,128)(2,1)}, u32[]{:S(2)}, u32[]{:S(2)}) collective-permute-start(bf16[640,1024]{1,0:T(8,128)(2,1)} %slice.104), channel_id=1, source_target_pairs={{4,0},{8,4},{12,8},{16,12},{20,16},{24,20},{28,24},{5,1},{9,5},{13... | collective-permute-start | bytes 3932168 | tf_op jit(solution)/shard_map/ppermute | solution.py:16
  51.3 78.8 %all-to-all-start.1 = ((bf16[192,4,1024]{2,0,1:T(8,128)(2,1)}), bf16[192,4,1024]{2,0,1:T(8,128)(2,1)}, u32[]{:S(2)}, u32[]{:S(2)}) async-start(bf16[192,4,1024]{2,0,1:T(8,128)(2,1)} %bitcast.51), calls=%async_computation.1 | async-start | bytes 3145728 | tf_op jit(solution)/shard_map/all_to_all | solution.py:58
  57.2 111.1 %collective-permute-start.2 = (bf16[768,1024]{1,0:T(8,128)(2,1)S(1)}, bf16[768,1024]{1,0:T(8,128)(2,1)}, u32[]{:S(2)}, u32[]{:S(2)}) collective-permute-start(bf16[768,1024]{1,0:T(8,128)(2,1)S(1)} %bitcast.42), channel_id=1, source_target_pairs={{0,4},{4,8},{8,12},{12,16},{16,20},{20,24},{24,28},{1,5},{5,9},{9,... | collective-permute-start | bytes 4718600 | tf_op jit(solution)/shard_map/ppermute | solution.py:16
  62.6 105.8 %collective-permute-start.3 = (bf16[640,1024]{1,0:T(8,128)(2,1)}, bf16[640,1024]{1,0:T(8,128)(2,1)}, u32[]{:S(2)}, u32[]{:S(2)}) collective-permute-start(bf16[640,1024]{1,0:T(8,128)(2,1)} %slice.107), channel_id=1, source_target_pairs={{4,0},{8,4},{12,8},{16,12},{20,16},{24,20},{28,24},{5,1},{9,5},{13... | collective-permute-start | bytes 3932168 | tf_op jit(solution)/shard_map/ppermute | solution.py:16
  130.1 4.2 %copy-start.1 = (bf16[2176,1024]{1,0:T(8,128)(2,1)S(1)}, bf16[2176,1024]{1,0:T(8,128)(2,1)}, u32[]{:S(2)}) copy-start(bf16[2176,1024]{1,0:T(8,128)(2,1)} %pad_maximum_fusion) | copy-start | bytes 13369348
  134.4 25.5 %copy-start = (f32[768,2176]{0,1:T(8,128)}, f32[768,2176]{0,1:T(8,128)S(1)}, u32[]{:S(2)}) copy-start(f32[768,2176]{0,1:T(8,128)S(1)} %get-tuple-element.8) | copy-start | bytes 20054020
  168.3 8.2 %slice-start.2 = ((s8[6684672]{0:T(1024)(128)(4,1)}), s8[4194304]{0:T(1024)(128)(4,1)S(1)}, s32[]{:S(2)}) async-start(s8[6684672]{0:T(1024)(128)(4,1)} %bitcast.49), calls=%async_computation.6 | async-start | bytes 8388608
  172.2 4.3 %slice-start.3 = ((s8[6684672]{0:T(1024)(128)(4,1)}), s8[2490368]{0:T(1024)(128)(4,1)S(1)}, s32[]{:S(2)}) async-start(s8[6684672]{0:T(1024)(128)(4,1)} %bitcast.49), calls=%async_computation.7 | async-start | bytes 4980736
  179.8 8.3 %slice-start = ((s8[6684672]{0:T(1024)(128)(4,1)}), s8[4194304]{0:T(1024)(128)(4,1)S(1)}, s32[]{:S(2)}) async-start(s8[6684672]{0:T(1024)(128)(4,1)} %bitcast.47), calls=%async_computation.4 | async-start | bytes 8388608
  183.8 4.3 %slice-start.1 = ((s8[6684672]{0:T(1024)(128)(4,1)}), s8[2490368]{0:T(1024)(128)(4,1)S(1)}, s32[]{:S(2)}) async-start(s8[6684672]{0:T(1024)(128)(4,1)} %bitcast.47), calls=%async_computation.5 | async-start | bytes 4980736
  204.5 5.3 %copy-start.6 = (s32[192]{0:T(256)S(1)}, s32[192]{0:T(256)}, u32[]{:S(2)}) copy-start(s32[192]{0:T(256)} %param.12) | copy-start | bytes 2308
  204.5 5.3 %copy-start.5 = (f32[192]{0:T(256)S(1)}, f32[192]{0:T(256)}, u32[]{:S(2)}) copy-start(f32[192]{0:T(256)} %param.13) | copy-start | bytes 2308
  206.2 64.7 %all-to-all-start.3 = ((bf16[4,192,1024]{2,1,0:T(8,128)(2,1)}), bf16[4,192,1024]{2,1,0:T(8,128)(2,1)S(1)}, u32[]{:S(2)}, u32[]{:S(2)}) async-start(bf16[4,192,1024]{2,1,0:T(8,128)(2,1)} %bitcast.17), calls=%async_computation.3 | async-start | bytes 3145728 | tf_op jit(solution)/shard_map/all_to_all | solution.py:100
  270.3 1.8 copy-start.7
where the time goes:
time: 273 us; the launch traced here: 272 us
  waiting for transfers between devices  90.8 us (33%)
  blocking collectives  60.4 us (22%)
  matrix products  59.3 us (22%)
  starting transfers between devices  29 us (11%)
  other arithmetic  19.2 us (7%)
  local copies, waits for them, and re-layouts  12.4 us (5%)
    ppermute x4, waiting for transfers between devices, shifted(): return lax.ppermute(block, axis, route)  62.6 us
    psum x1, blocking collectives, per_device(): counts, sums = lax.psum((counts, sums), ('seq', 'head'))  60.4 us
    dot_general x8, matrix products, attend(): lax.dot_general(query_head, key_head, (((1,), (1,)), ((), ())), preferred...  37.1 us
    dot_general x8, matrix products, attend(): jnp.dot(weights.astype(jnp.bfloat16), value_head, preferred_element_type=...  22.2 us
    all_to_all x1, waiting for transfers between devices, per_device(): lax.all_to_all(key_rows, 'head', split_axis=1, concat_axis=0, tiled=True)  18.7 us
    ppermute x4, starting transfers between devices, shifted(): return lax.ppermute(block, axis, route)  13.3 us
    reduce_sum x8, other arithmetic, attend(): total = jnp.sum(weights, axis=1, keepdims=True)  10.9 us
    all_to_all x1, waiting for transfers between devices, per_device(): lax.all_to_all(values, 'head', split_axis=1, concat_axis=0, tiled=True)  9.44 us
  transfers between devices with their start and end apart: 8, of which 4 were waited for; matrix products, arithmetic and copies ran while one was open for 18% of the time, Pallas kernels for 0%

commit v1 on v0

v1 whole, which is shorter than its diff:
```python
import functools
import math

import jax
import jax.numpy as jnp
from jax import lax
from jax.experimental import pallas as pl
from jax.experimental.pallas import tpu as pltpu
from jax.sharding import Mesh, PartitionSpec as P

HEAD_DIM = 128
DOC_MEAN = 384
DOC_MOST = 704
IMG_LEN = 576
LEAST = -1e30
GRAIN = 64


def round_up(count, grain):
    return -(-count // grain) * grain


def shifted(block, axis, distance):
    devices = range(lax.axis_size(axis))
    route = [(i - distance, i) for i in devices if i - distance in devices]
    return lax.ppermute(block, axis, route)


def summed(totals, axis):
    size = lax.axis_size(axis)
    if size & (size - 1):
        return lax.psum(totals, axis)
    distance = 1
    while distance < size:
        totals = totals + lax.ppermute(totals, axis, [(i, i ^ distance) for i in range(size)])
        distance *= 2
    return totals


def attend_kernel(
    first_ref, count_ref, low_ref, span_ref, q_ref,
    k_back_ref, k_own_ref, k_ahead_ref, v_back_ref, v_own_ref, v_ahead_ref,
    out_ref, keys, mixed, scores, top, gathered, *, heads, width,
):
    step = pl.program_id(0)
    rows = q_ref.shape[0]
    window = keys.shape[0]
    back = k_back_ref.shape[0]
    own = k_own_ref.shape[0]
    ahead = k_ahead_ref.shape[0]
    factor = HEAD_DIM ** (-0.5) * math.log2(math.e)

    @pl.when(step == 0)
    def _():
        pieces = ((0, back, k_back_ref, v_back_ref), (back, own, k_own_ref, v_own_ref),
                  (back + own, ahead, k_ahead_ref, v_ahead_ref))
        ones = jnp.ones((window, HEAD_DIM), mixed.dtype)
        for start, length, key_part, value_part in pieces:
            keys[start:start + length, :] = key_part[...]
            for head in range(heads):
                lower = head * HEAD_DIM
                mixed[start:start + length, 2 * lower:2 * lower + HEAD_DIM] = (
                    value_part[:, lower:lower + HEAD_DIM])
        rest = window - back - own - ahead
        keys[window - rest:, :] = jnp.zeros((rest, keys.shape[1]), keys.dtype)
        for head in range(heads):
            lower = head * HEAD_DIM
            mixed[window - rest:, 2 * lower:2 * lower + HEAD_DIM] = jnp.zeros((rest, HEAD_DIM), mixed.dtype)
            mixed[:, 2 * lower + HEAD_DIM:2 * lower + 2 * HEAD_DIM] = ones

    first = first_ref[step]
    count = count_ref[step]
    places = lax.broadcasted_iota(jnp.int32, (rows, width), 1)
    distance = places - low_ref[...]
    span = span_ref[...]

    top[...] = jnp.full(top.shape, LEAST, jnp.float32)

    def score(tile, carry):
        start = pl.multiple_of(first + tile * width, GRAIN)
        away = distance + start
        allowed = (away >= 0) & (away < span)
        for head in range(heads):
            lower = head * HEAD_DIM
            part = lax.dot_general(
                q_ref[:, lower:lower + HEAD_DIM], keys[pl.ds(start, width), lower:lower + HEAD_DIM],
                (((1,), (1,)), ((), ())), preferred_element_type=jnp.float32)
            part = jnp.where(allowed, part, LEAST)
            scores[tile, head] = part
            best = top[head]
            for chunk in range(width // HEAD_DIM):
                best = jnp.maximum(best, part[:, chunk * HEAD_DIM:(chunk + 1) * HEAD_DIM])
            top[head] = best
        return carry

    lax.fori_loop(0, count, score, 0)
    for head in range(heads):
        top[head] = jnp.broadcast_to(jnp.max(top[head], axis=1, keepdims=True), top.shape[1:])
    gathered[...] = jnp.zeros_like(gathered)

    def mix(tile, carry):
        start = pl.multiple_of(first + tile * width, GRAIN)
        for head in range(heads):
            lower = 2 * head * HEAD_DIM
            best = jnp.concatenate([top[head]] * (width // HEAD_DIM), axis=1)
            weights = jnp.exp2((scores[tile, head] - best) * factor)
            gathered[head] += jnp.dot(
                weights.astype(jnp.bfloat16), mixed[pl.ds(start, width), lower:lower + 2 * HEAD_DIM],
                preferred_element_type=jnp.float32)
        return carry

    lax.fori_loop(0, count, mix, 0)
    for head in range(heads):
        lower = head * HEAD_DIM
        result = gathered[head]
        out_ref[:, lower:lower + HEAD_DIM] = (
            result[:, :HEAD_DIM] / result[:, HEAD_DIM:]).astype(out_ref.dtype)


def attend(first, count, low, span, queries, key_parts, value_parts, tile_rows, width):
    rows, columns = queries.shape
    heads = columns // HEAD_DIM
    held = sum(part.shape[0] for part in key_parts)
    window = held + width
    most = -(-(GRAIN + DOC_MOST + tile_rows + IMG_LEN) // width)
    whole = [pl.BlockSpec(part.shape, lambda i, *_: (0, 0)) for part in (*key_parts, *value_parts)]
    tiles = [pl.BlockSpec((tile_rows, size), lambda i, *_: (i, 0)) for size in (1, 1, columns)]
    return pl.pallas_call(
        functools.partial(attend_kernel, heads=heads, width=width),
        out_shape=jax.ShapeDtypeStruct((rows, columns), queries.dtype),
        grid_spec=pltpu.PrefetchScalarGridSpec(
            num_scalar_prefetch=2, grid=(rows // tile_rows,),
            in_specs=tiles + whole,
            out_specs=pl.BlockSpec((tile_rows, columns), lambda i, *_: (i, 0)),
            scratch_shapes=[
                pltpu.VMEM((window, columns), queries.dtype),
                pltpu.VMEM((window, 2 * columns), queries.dtype),
                pltpu.VMEM((most, heads, tile_rows, width), jnp.float32),
                pltpu.VMEM((heads, tile_rows, HEAD_DIM), jnp.float32),
                pltpu.VMEM((heads, tile_rows, 2 * HEAD_DIM), jnp.float32),
            ]),
        compiler_params=pltpu.CompilerParams(
            dimension_semantics=("arbitrary",), vmem_limit_bytes=56 * 2**20),
        cost_estimate=pl.CostEstimate(
            flops=4 * rows * 640 * columns, bytes_accessed=2 * (2 * rows + 2 * held) * columns,
            transcendentals=rows * 640 * heads),
        name="attend",
    )(first, count, low, span, queries, *key_parts, *value_parts)


def whole_step(queries, key_rows, values, doc_ids, image_flags, labels, token_loss):
    group = ("pair", "head")
    members = lax.axis_size("pair") * lax.axis_size("head")
    local_rows = queries.shape[0]
    rows = local_rows * members
    tile_rows, width = 256, 256

    exchange = functools.partial(lax.all_to_all, axis_name=group, split_axis=1, concat_axis=0, tiled=True)
    back = round_up(DOC_MOST - 1, GRAIN)
    ahead = round_up(IMG_LEN - 1, GRAIN)
    keys = exchange(key_rows)
    vals = exchange(values)
    quer = exchange(queries)
    key_back = shifted(keys[rows - back:], "outer", 1)
    key_ahead = shifted(keys[:ahead], "outer", -1)
    value_back = shifted(vals[rows - back:], "outer", 1)
    value_ahead = shifted(vals[:ahead], "outer", -1)
    key_parts = (key_back, keys, key_ahead)
    value_parts = (value_back, vals, value_ahead)

    documents = doc_ids.shape[0] // DOC_MEAN
    numbers = jnp.arange(documents, dtype=jnp.int32)[:, None]
    places = jnp.arange(doc_ids.shape[0], dtype=jnp.int32)[None, :]
    starts = jnp.sum((doc_ids[None, :] < numbers).astype(jnp.int32), axis=1, keepdims=True)
    image = (doc_ids[None, :] == numbers) & (image_flags[None, :] == 1)
    image_ends = jnp.max(jnp.where(image, places + 1, 0), axis=1, keepdims=True)
    block_start = lax.axis_index("outer") * rows
    block_docs = lax.dynamic_slice_in_dim(doc_ids, block_start, rows)[None, :]
    block_flags = lax.dynamic_slice_in_dim(image_flags, block_start, rows)
    own = block_docs == numbers
    low = jnp.sum(jnp.where(own, starts, 0), axis=0)
    image_high = jnp.sum(jnp.where(own, image_ends, 0), axis=0)
    high = jnp.where(block_flags == 1, image_high, block_start + jnp.arange(rows, dtype=jnp.int32) + 1)
    low = low - (block_start - back)
    high = high - (block_start - back)
    first = low[::tile_rows] // GRAIN * GRAIN
    last = jnp.max(high.reshape(-1, tile_rows), axis=1)
    count = (last - first + width - 1) // width

    attended = attend(first, count, low[:, None], (high - low)[:, None], quer, key_parts, value_parts, tile_rows, width)
    output = lax.all_to_all(attended, group, split_axis=0, concat_axis=1, tiled=True)

    row_start = block_start + (lax.axis_index("pair") * lax.axis_size("head") + lax.axis_index("head")) * local_rows
    local_docs = lax.dynamic_slice_in_dim(doc_ids, row_start, local_rows)
    member = (local_docs[:, None] == numbers.T) & (labels[:, None] >= 0)
    counts = jnp.sum(member.astype(jnp.float32), axis=0)
    sums = jnp.sum(jnp.where(member, token_loss[:, None], jnp.float32(0.0)), axis=0)
    totals = jnp.stack([counts, sums])
    for axis in ("head", "pair", "outer"):
        totals = summed(totals, axis)
    counts, sums = totals
    return (output, counts, sums / jnp.maximum(counts, jnp.float32(1.0)))


def solution(mesh):
    blocks, heads = mesh.shape["seq"], mesh.shape["head"]
    pair = 2 if blocks % 2 == 0 else 1
    fine = Mesh(mesh.devices.reshape(blocks // pair, pair, heads), ("outer", "pair", "head"))
    tokens = ("outer", "pair", "head")
    in_specs = (P(tokens, None), P(tokens, None), P(tokens, None), P(), P(), P(tokens), P(tokens))
    out_specs = (P(tokens, None), P(), P())
    return jax.shard_map(whole_step, mesh=fine, in_specs=in_specs, out_specs=out_specs, check_vma=False)
```

time: 273 us -> 158 us (0.58)
  blocking collectives: 60.4 us -> 0 us
  matrix products: 59.3 us -> 0 us
  Pallas kernels: 0 us -> 19.5 us
  other arithmetic: 19.2 us -> 1.83 us
  starting transfers between devices: 29 us -> 36.1 us
  waiting for transfers between devices: 90.8 us -> 85.2 us
    psum x1 -> x0, blocking collectives: 60.4 us -> none  [per_device(): counts, sums = lax.psum((counts, sums), ('seq', 'head'))]
    dot_general x16 -> x0, matrix products: 59.3 us -> none  [the longest x8 37.1 us: attend(): lax.dot_general(query_head, key_head, (((1,), (1,)), ((), ())), preferred...]
    ppermute x4, waiting for transfers between devices: 62.6 us -> 19.4 us  [shifted(): return lax.ppermute(block, axis, route)]
    ppermute x0 -> x5, waiting for transfers between devices: none -> 23.8 us  [summed(): lax.ppermute(totals, axis, [(i, i ^ distance) for i in range(size)])]
    pallas_call x0 -> x1, Pallas kernels: none -> 19.5 us  [attend(): pl.pallas_call(functools.partial(attend_kernel, heads=heads, width=width)...]
    all_to_all x4, waiting for transfers between devices: 28.2 us -> 42 us  [the longest x1 19.7 us: whole_step(): keys = exchange(key_rows)]
    reduce_sum x9 -> x2, other arithmetic: 11 us -> 0.23 us  [the longest x1 0.12 us: whole_step(): counts = jnp.sum(member.astype(jnp.float32), axis=0)]
    ppermute x0 -> x5, starting transfers between devices: none -> 8.37 us  [summed(): lax.ppermute(totals, axis, [(i, i ^ distance) for i in range(size)])]
  transfers between devices with their start and end apart: 8 -> 13, of which waited for: 4 -> 10; matrix products, arithmetic and copies ran while one was open for 18% -> 7% of each run, Pallas kernels for 0% -> 0%
where the time goes in v1:
time: 158 us
  waiting for transfers between devices  85.2 us (54%)
  starting transfers between devices  36.1 us (23%)
  Pallas kernels  19.5 us (12%)
  local copies, waits for them, and re-layouts  14.3 us (9%)
  other arithmetic  1.83 us (1%)
    ppermute x5, waiting for transfers between devices, summed(): lax.ppermute(totals, axis, [(i, i ^ distance) for i in range(size)])  23.8 us
    all_to_all x1, waiting for transfers between devices, whole_step(): keys = exchange(key_rows)  19.7 us
    pallas_call x1, Pallas kernels, attend(): pl.pallas_call(functools.partial(attend_kernel, heads=heads, width=width)...  19.5 us
    ppermute x4, waiting for transfers between devices, shifted(): return lax.ppermute(block, axis, route)  19.4 us
    all_to_all x1, waiting for transfers between devices, whole_step(): vals = exchange(values)  18.2 us
    ppermute x4, starting transfers between devices, shifted(): return lax.ppermute(block, axis, route)  10.4 us
    ppermute x5, starting transfers between devices, summed(): lax.ppermute(totals, axis, [(i, i ^ distance) for i in range(size)])  8.37 us
    all_to_all x1, starting transfers between devices, whole_step(): keys = exchange(key_rows)  5.33 us
  transfers between devices with their start and end apart: 13, of which 10 were waited for; matrix products, arithmetic and copies ran while one was open for 7% of the time, Pallas kernels for 0%

profile of v1, /device:TPU:0, one launch (start us, length us, event | category | flops | bytes accessed | tf_op | source)
XLA Modules:
  0.0 157.6 jit_solution(12210297372576422947)
XLA Ops:
  0.6 2.7 %copy.34 = bf16[24,8,8,512]{3,2,0,1:T(8,128)(2,1)} copy(bf16[24,8,8,512]{3,2,1,0:T(8,128)(2,1)} %bitcast.44) | data formatting | bytes 3145728 | tf_op jit(solution)/shard_map/all_to_all | solution.py:161
  3.3 5.3 %all-to-all-start.1 = ((bf16[192,8,512]{2,0,1:T(8,128)(2,1)}), bf16[192,8,512]{2,0,1:T(8,128)(2,1)S(1)}, u32[]{:S(2)}, u32[]{:S(2)}) async-start(bf16[192,8,512]{2,0,1:T(8,128)(2,1)} %bitcast.32), calls=%async_computation.1 | async-start | bytes 3145728 | tf_op jit(solution)/shard_map/all_to_all | solution.py:161
  8.7 1.3 copy.33
  10.0 19.7 %all-to-all-done.1 = bf16[192,8,512]{2,0,1:T(8,128)(2,1)S(1)} async-done(((bf16[192,8,512]{2,0,1:T(8,128)(2,1)}), bf16[192,8,512]{2,0,1:T(8,128)(2,1)S(1)}, u32[]{:S(2)}, u32[]{:S(2)}) %all-to-all-start.1) | async-done | bytes 1572896 | tf_op jit(solution)/shard_map/all_to_all | solution.py:161
  29.7 3.6 %all-to-all-start.2 = ((bf16[192,8,512]{2,0,1:T(8,128)(2,1)}), bf16[192,8,512]{2,0,1:T(8,128)(2,1)S(1)}, u32[]{:S(2)}, u32[]{:S(2)}) async-start(bf16[192,8,512]{2,0,1:T(8,128)(2,1)} %bitcast.42), calls=%async_computation.2 | async-start | bytes 3145728 | tf_op jit(solution)/shard_map/all_to_all | solution.py:162
  33.2 2.7 %copy.35 = bf16[24,8,8,512]{3,2,0,1:T(8,128)(2,1)} copy(bf16[24,8,8,512]{3,2,1,0:T(8,128)(2,1)} %bitcast.46) | data formatting | bytes 3145728 | tf_op jit(solution)/shard_map/all_to_all | solution.py:163
  36.0 18.2 %all-to-all-done.2 = bf16[192,8,512]{2,0,1:T(8,128)(2,1)S(1)} async-done(((bf16[192,8,512]{2,0,1:T(8,128)(2,1)}), bf16[192,8,512]{2,0,1:T(8,128)(2,1)S(1)}, u32[]{:S(2)}, u32[]{:S(2)}) %all-to-all-start.2) | async-done | bytes 1572896 | tf_op jit(solution)/shard_map/all_to_all | solution.py:162
  54.2 4.4 %all-to-all-start = ((bf16[192,8,512]{2,0,1:T(8,128)(2,1)}), bf16[192,8,512]{2,0,1:T(8,128)(2,1)}, u32[]{:S(2)}, u32[]{:S(2)}) async-start(bf16[192,8,512]{2,0,1:T(8,128)(2,1)} %bitcast.41), calls=%async_computation | async-start | bytes 3145728 | tf_op jit(solution)/shard_map/all_to_all | solution.py:163
  59.6 4.3 %collective-permute-start = (bf16[704,512]{1,0:T(8,128)(2,1)}, bf16[704,512]{1,0:T(8,128)(2,1)}, u32[]{:S(2)}, u32[]{:S(2)}) collective-permute-start(bf16[704,512]{1,0:T(8,128)(2,1)} %slice.28), channel_id=1, source_target_pairs={{0,8},{8,16},{16,24},{1,9},{9,17},{17,25},{2,10},{10,18},{18,26},{... | collective-permute-start | bytes 2162696 | tf_op jit(solution)/shard_map/ppermute | solution.py:26
  64.9 3.5 %collective-permute-start.2 = (bf16[704,512]{1,0:T(8,128)(2,1)}, bf16[704,512]{1,0:T(8,128)(2,1)}, u32[]{:S(2)}, u32[]{:S(2)}) collective-permute-start(bf16[704,512]{1,0:T(8,128)(2,1)} %slice.30), channel_id=1, source_target_pairs={{0,8},{8,16},{16,24},{1,9},{9,17},{17,25},{2,10},{10,18},{18,26},{... | collective-permute-start | bytes 2162696 | tf_op jit(solution)/shard_map/ppermute | solution.py:26
  75.6 4.0 %all-to-all-done = bf16[192,8,512]{2,0,1:T(8,128)(2,1)} async-done(((bf16[192,8,512]{2,0,1:T(8,128)(2,1)}), bf16[192,8,512]{2,0,1:T(8,128)(2,1)}, u32[]{:S(2)}, u32[]{:S(2)}) %all-to-all-start) | async-done | bytes 1572896 | tf_op jit(solution)/shard_map/all_to_all | solution.py:163
  79.6 7.9 %collective-permute-done.1.k_ahead_ref = bf16[576,512]{1,0:T(8,128)(2,1)S(1)} collective-permute-done((bf16[576,512]{1,0:T(8,128)(2,1)}, bf16[576,512]{1,0:T(8,128)(2,1)S(1)}, u32[]{:S(2)}, u32[]{:S(2)}) %collective-permute-start.1) | collective-permute-done | bytes 589856 | tf_op jit(solution)/shard_map/ppermute | solution.py:26
  87.6 11.5 %collective-permute-done.3.v_ahead_ref = bf16[576,512]{1,0:T(8,128)(2,1)S(1)} collective-permute-done((bf16[576,512]{1,0:T(8,128)(2,1)S(1)}, bf16[576,512]{1,0:T(8,128)(2,1)S(1)}, u32[]{:S(2)}, u32[]{:S(2)}) %collective-permute-start.3) | collective-permute-done | bytes 589856 | tf_op jit(solution)/shard_map/ppermute | solution.py:26
  99.8 19.5 %attend.1 = bf16[1536,512]{1,0:T(8,128)(2,1)} custom-call(s32[6]{0:T(128)} %get-tuple-element.15.first_ref, s32[6]{0:T(128)} %get-tuple-element.14.count_ref, s32[1536,1]{1,0:T(8,128)} %sub.53.low_ref, s32[1536,1]{1,0:T(8,128)} %broadcast_in_dim.65.span_ref, bf16[1536,512]{1,0:T(8,128)(2,1)} %bitcast.1.q_ref, ...), custom_call_target="tpu_custom_call" | custom-call | flops 2013265920 | bytes 8912896 | tf_op jit(solution)/shard_map/attend/pallas_call | solution.py:128
  119.3 4.0 %all-to-all-start.3 = ((bf16[8,192,512]{2,1,0:T(8,128)(2,1)}), bf16[8,192,512]{2,1,0:T(8,128)(2,1)S(1)}, u32[]{:S(2)}, u32[]{:S(2)}) async-start(bf16[8,192,512]{2,1,0:T(8,128)(2,1)} %bitcast.43), calls=%async_computation.3 | async-start | bytes 3145728 | tf_op jit(solution)/shard_map/all_to_all | solution.py:191
  125.0 1.9 %collective-permute-start.5 = (f32[2,16]{1,0:T(2,128)S(1)}, f32[2,16]{1,0:T(2,128)S(1)}, u32[]{:S(2)}, u32[]{:S(2)}) collective-permute-start(f32[2,16]{1,0:T(2,128)S(1)} %fusion.3), channel_id=1, source_target_pairs={{0,2},{1,3},{2,0},{3,1},{4,6},{5,7},{6,4},{7,5},{8,10},{9,11},{10,... | collective-permute-start | bytes 392 | tf_op jit(solution)/shard_map/ppermute | solution.py:35
  126.9 16.6 %collective-permute-done.5 = f32[2,16]{1,0:T(2,128)S(1)} collective-permute-done((f32[2,16]{1,0:T(2,128)S(1)}, f32[2,16]{1,0:T(2,128)S(1)}, u32[]{:S(2)}, u32[]{:S(2)}) %collective-permute-start.5) | collective-permute-done | bytes 160 | tf_op jit(solution)/shard_map/ppermute | solution.py:35
  143.5 1.5 collective-permute-start.6
  145.0 2.1 %collective-permute-done.6 = f32[2,16]{1,0:T(2,128)S(1)} collective-permute-done((f32[2,16]{1,0:T(2,128)S(1)}, f32[2,16]{1,0:T(2,128)S(1)}, u32[]{:S(2)}, u32[]{:S(2)}) %collective-permute-start.6) | collective-permute-done | bytes 160 | tf_op jit(solution)/shard_map/ppermute | solution.py:35
  147.1 2.6 %collective-permute-start.7 = (f32[2,16]{1,0:T(2,128)S(1)}, f32[2,16]{1,0:T(2,128)S(1)}, u32[]{:S(2)}, u32[]{:S(2)}) collective-permute-start(f32[2,16]{1,0:T(2,128)S(1)} %add.62), channel_id=1, source_target_pairs={{0,8},{8,0},{16,24},{24,16},{1,9},{9,1},{17,25},{25,17},{2,10},{10... | collective-permute-start | bytes 392 | tf_op jit(solution)/shard_map/ppermute | solution.py:35
  149.7 1.6 collective-permute-done.7
  151.3 1.7 %collective-permute-start.8 = (f32[2,16]{1,0:T(2,128)S(1)}, f32[2,16]{1,0:T(2,128)S(1)}, u32[]{:S(2)}, u32[]{:S(2)}) collective-permute-start(f32[2,16]{1,0:T(2,128)S(1)} %add.63), channel_id=1, source_target_pairs={{0,16},{8,24},{16,0},{24,8},{1,17},{9,25},{17,1},{25,9},{2,18},{10... | collective-permute-start | bytes 392 | tf_op jit(solution)/shard_map/ppermute | solution.py:35
  153.0 2.7 %collective-permute-done.8 = f32[2,16]{1,0:T(2,128)S(1)} collective-permute-done((f32[2,16]{1,0:T(2,128)S(1)}, f32[2,16]{1,0:T(2,128)S(1)}, u32[]{:S(2)}, u32[]{:S(2)}) %collective-permute-start.8) | collective-permute-done | bytes 160 | tf_op jit(solution)/shard_map/ppermute | solution.py:35
  156.3 1.3 copy.29
  (51 shorter events, 12.1 us)
Async XLA Ops:
  3.3 5.3 %copy-start.2 = (bf16[192,4096]{1,0:T(8,128)(2,1)S(1)}, bf16[192,4096]{1,0:T(8,128)(2,1)}, u32[]{:S(2)}) copy-start(bf16[192,4096]{1,0:T(8,128)(2,1)} %param.9) | copy-start | bytes 4718596
  3.3 26.3 %all-to-all-start.1 = ((bf16[192,8,512]{2,0,1:T(8,128)(2,1)}), bf16[192,8,512]{2,0,1:T(8,128)(2,1)S(1)}, u32[]{:S(2)}, u32[]{:S(2)}) async-start(bf16[192,8,512]{2,0,1:T(8,128)(2,1)} %bitcast.32), calls=%async_computation.1 | async-start | bytes 3145728 | tf_op jit(solution)/shard_map/all_to_all | solution.py:161
  29.7 38.8 %copy-start = (bf16[192,8,512]{2,0,1:T(8,128)(2,1)}, bf16[192,8,512]{2,0,1:T(8,128)(2,1)S(1)}, u32[]{:S(2)}) copy-start(bf16[192,8,512]{2,0,1:T(8,128)(2,1)S(1)} %all-to-all-done.1) | copy-start | bytes 4718596
  29.7 24.5 %all-to-all-start.2 = ((bf16[192,8,512]{2,0,1:T(8,128)(2,1)}), bf16[192,8,512]{2,0,1:T(8,128)(2,1)S(1)}, u32[]{:S(2)}, u32[]{:S(2)}) async-start(bf16[192,8,512]{2,0,1:T(8,128)(2,1)} %bitcast.42), calls=%async_computation.2 | async-start | bytes 3145728 | tf_op jit(solution)/shard_map/all_to_all | solution.py:162
  54.2 16.4 %copy-start.1 = (bf16[192,8,512]{2,0,1:T(8,128)(2,1)}, bf16[192,8,512]{2,0,1:T(8,128)(2,1)S(1)}, u32[]{:S(2)}) copy-start(bf16[192,8,512]{2,0,1:T(8,128)(2,1)S(1)} %all-to-all-done.2) | copy-start | bytes 4718596
  54.2 4.4 %copy-start.6 = (s32[6144]{0:T(1024)S(1)}, s32[6144]{0:T(1024)}, u32[]{:S(2)}) copy-start(s32[6144]{0:T(1024)} %param.11) | copy-start | bytes 73732
  54.2 25.4 %all-to-all-start = ((bf16[192,8,512]{2,0,1:T(8,128)(2,1)}), bf16[192,8,512]{2,0,1:T(8,128)(2,1)}, u32[]{:S(2)}, u32[]{:S(2)}) async-start(bf16[192,8,512]{2,0,1:T(8,128)(2,1)} %bitcast.41), calls=%async_computation | async-start | bytes 3145728 | tf_op jit(solution)/shard_map/all_to_all | solution.py:163
  59.6 39.4 %collective-permute-start = (bf16[704,512]{1,0:T(8,128)(2,1)}, bf16[704,512]{1,0:T(8,128)(2,1)}, u32[]{:S(2)}, u32[]{:S(2)}) collective-permute-start(bf16[704,512]{1,0:T(8,128)(2,1)} %slice.28), channel_id=1, source_target_pairs={{0,8},{8,16},{16,24},{1,9},{9,17},{17,25},{2,10},{10,18},{18,26},{... | collective-permute-start | bytes 2162696 | tf_op jit(solution)/shard_map/ppermute | solution.py:26
  63.9 8.0 %copy-start.5 = (s32[6144]{0:T(1024)S(1)}, s32[6144]{0:T(1024)}, u32[]{:S(2)}) copy-start(s32[6144]{0:T(1024)} %param.10) | copy-start | bytes 73732
  64.9 34.1 %collective-permute-start.2 = (bf16[704,512]{1,0:T(8,128)(2,1)}, bf16[704,512]{1,0:T(8,128)(2,1)}, u32[]{:S(2)}, u32[]{:S(2)}) collective-permute-start(bf16[704,512]{1,0:T(8,128)(2,1)} %slice.30), channel_id=1, source_target_pairs={{0,8},{8,16},{16,24},{1,9},{9,17},{17,25},{2,10},{10,18},{18,26},{... | collective-permute-start | bytes 2162696 | tf_op jit(solution)/shard_map/ppermute | solution.py:26
  69.3 18.3 %collective-permute-start.1 = (bf16[576,512]{1,0:T(8,128)(2,1)}, bf16[576,512]{1,0:T(8,128)(2,1)S(1)}, u32[]{:S(2)}, u32[]{:S(2)}) collective-permute-start(bf16[576,512]{1,0:T(8,128)(2,1)} %bitcast.4), channel_id=1, source_target_pairs={{8,0},{16,8},{24,16},{9,1},{17,9},{25,17},{10,2},{18,10},{26,18},{... | collective-permute-start | bytes 1769480 | tf_op jit(solution)/shard_map/ppermute | solution.py:26
  70.6 28.4 %collective-permute-start.3 = (bf16[576,512]{1,0:T(8,128)(2,1)S(1)}, bf16[576,512]{1,0:T(8,128)(2,1)S(1)}, u32[]{:S(2)}, u32[]{:S(2)}) collective-permute-start(bf16[576,512]{1,0:T(8,128)(2,1)S(1)} %bitcast.48), channel_id=1, source_target_pairs={{8,0},{16,8},{24,16},{9,1},{17,9},{25,17},{10,2},{18,10},{26,18},{... | collective-permute-start | bytes 1769480 | tf_op jit(solution)/shard_map/ppermute | solution.py:26
  87.6 11.5 %copy-start.3 = (bf16[576,512]{1,0:T(8,128)(2,1)}, bf16[576,512]{1,0:T(8,128)(2,1)S(1)}, u32[]{:S(2)}) copy-start(bf16[576,512]{1,0:T(8,128)(2,1)S(1)} %collective-permute-done.1.k_ahead_ref) | copy-start | bytes 1769476
  99.0 0.8 copy-start.4
  119.3 4.1 %copy-start.8 = (s32[192]{0:T(256)S(1)}, s32[192]{0:T(256)}, u32[]{:S(2)}) copy-start(s32[192]{0:T(256)} %param.12) | copy-start | bytes 2308
  119.3 4.1 %copy-start.7 = (f32[192]{0:T(256)S(1)}, f32[192]{0:T(256)}, u32[]{:S(2)}) copy-start(f32[192]{0:T(256)} %param.13) | copy-start | bytes 2308
  119.3 36.9 %all-to-all-start.3 = ((bf16[8,192,512]{2,1,0:T(8,128)(2,1)}), bf16[8,192,512]{2,1,0:T(8,128)(2,1)S(1)}, u32[]{:S(2)}, u32[]{:S(2)}) async-start(bf16[8,192,512]{2,1,0:T(8,128)(2,1)} %bitcast.43), calls=%async_computation.3 | async-start | bytes 3145728 | tf_op jit(solution)/shard_map/all_to_all | solution.py:191
  123.5 1.4 collective-permute-start.4
  125.0 18.5 %collective-permute-start.5 = (f32[2,16]{1,0:T(2,128)S(1)}, f32[2,16]{1,0:T(2,128)S(1)}, u32[]{:S(2)}, u32[]{:S(2)}) collective-permute-start(f32[2,16]{1,0:T(2,128)S(1)} %fusion.3), channel_id=1, source_target_pairs={{0,2},{1,3},{2,0},{3,1},{4,6},{5,7},{6,4},{7,5},{8,10},{9,11},{10,... | collective-permute-start | bytes 392 | tf_op jit(solution)/shard_map/ppermute | solution.py:35
  143.5 3.6 %collective-permute-start.6 = (f32[2,16]{1,0:T(2,128)S(1)}, f32[2,16]{1,0:T(2,128)S(1)}, u32[]{:S(2)}, u32[]{:S(2)}) collective-permute-start(f32[2,16]{1,0:T(2,128)S(1)} %fusion.6), channel_id=1, source_target_pairs={{0,4},{4,0},{1,5},{5,1},{2,6},{6,2},{3,7},{7,3},{8,12},{12,8},{9,1... | collective-permute-start | bytes 392 | tf_op jit(solution)/shard_map/ppermute | solution.py:35
  147.1 4.2 %collective-permute-start.7 = (f32[2,16]{1,0:T(2,128)S(1)}, f32[2,16]{1,0:T(2,128)S(1)}, u32[]{:S(2)}, u32[]{:S(2)}) collective-permute-start(f32[2,16]{1,0:T(2,128)S(1)} %add.62), channel_id=1, source_target_pairs={{0,8},{8,0},{16,24},{24,16},{1,9},{9,1},{17,25},{25,17},{2,10},{10... | collective-permute-start | bytes 392 | tf_op jit(solution)/shard_map/ppermute | solution.py:35
  151.3 4.5 %collective-permute-start.8 = (f32[2,16]{1,0:T(2,128)S(1)}, f32[2,16]{1,0:T(2,128)S(1)}, u32[]{:S(2)}, u32[]{:S(2)}) collective-permute-start(f32[2,16]{1,0:T(2,128)S(1)} %add.63), channel_id=1, source_target_pairs={{0,16},{8,24},{16,0},{24,8},{1,17},{9,25},{17,1},{25,9},{2,18},{10... | collective-permute-start | bytes 392 | tf_op jit(solution)/shard_map/ppermute | solution.py:35

commit v2 on v1

v2 whole, which is shorter than its diff:
```python
import functools
import math

import jax
import jax.numpy as jnp
from jax import lax
from jax.experimental import pallas as pl
from jax.experimental.pallas import tpu as pltpu
from jax.sharding import Mesh, PartitionSpec as P

HEAD_DIM = 128
DOC_MEAN = 384
DOC_MOST = 704
IMG_LEN = 576
LEAST = -1e30
GRAIN = 16
HALO_GRAIN = 64
HALVES = 2
VMEM_LIMIT = 20 * 2**20


def round_up(count, grain):
    return -(-count // grain) * grain


def shifted(block, axis, distance):
    devices = range(lax.axis_size(axis))
    route = [(i - distance, i) for i in devices if i - distance in devices]
    return lax.ppermute(block, axis, route)


def summed(totals, axis):
    size = lax.axis_size(axis)
    if size & (size - 1):
        return lax.psum(totals, axis)
    distance = 1
    while distance < size:
        totals = totals + lax.ppermute(totals, axis, [(i, i ^ distance) for i in range(size)])
        distance *= 2
    return totals


def column(ref, step, rows):
    lines = rows // HEAD_DIM
    tall = [
        jnp.broadcast_to(ref[pl.ds(step * lines + line, 1), :], (HEAD_DIM, HEAD_DIM)).T
        for line in range(lines)
    ]
    return jnp.concatenate(tall, axis=0)


def attend_kernel(
    plan_ref, low_ref, span_ref, queries_ref, back_ref, own_ref, ahead_ref,
    out_ref, plan, query, keys, vals, scores, top, gathered, ready, sent, came, *, heads, width, common, place,
):
    step = pl.program_id(0)
    rows = ready.shape[1]
    steps = out_ref.shape[0] // rows
    window = keys.shape[0]
    factor = HEAD_DIM ** (-0.5) * math.log2(math.e)

    back, own, ahead = back_ref.shape[0], own_ref.shape[0], ahead_ref.shape[0]
    held = back + own + ahead
    columns = keys.shape[1]

    def halo(side, target):
        lower = side * columns
        return [
            pltpu.make_async_copy(
                part.at[:, lower:lower + columns], target.at[start:start + part.shape[0], :],
                came.at[2 + 2 * side + index])
            for index, (part, start) in enumerate(((back_ref, 0), (ahead_ref, back + own)))
        ]

    needs = [
        pltpu.make_async_copy(plan_ref, plan, came.at[0]),
        pltpu.make_async_copy(
            queries_ref.at[:, place * columns:(place + 1) * columns], query, came.at[1]),
    ] + halo(0, keys)
    rest = halo(1, vals)

    @pl.when(step == 0)
    def _():
        for move in needs + rest:
            move.start()
        for side, target in enumerate((keys, vals)):
            lower = (2 * place + side) * columns
            target[back:back + own, :] = own_ref[:, lower:lower + columns]
            target[held:, :] = jnp.zeros((window - held, columns), target.dtype)
        for move in needs:
            move.wait()

    first = plan[0, step]
    count = plan[1, step]
    tile = pl.ds(pl.multiple_of(step * rows, rows), rows)
    lanes = lax.broadcasted_iota(jnp.int32, (rows, HEAD_DIM), 1)
    above = lanes - column(low_ref, step, rows)
    below = above - column(span_ref, step, rows)

    def score(turn, tiles, fresh):
        start = pl.multiple_of(first + turn * width, GRAIN)
        for head in range(heads):
            lower = head * HEAD_DIM
            part = lax.dot_general(
                query[tile, lower:lower + HEAD_DIM], keys[pl.ds(start, tiles * width), lower:lower + HEAD_DIM],
                (((1,), (1,)), ((), ())), preferred_element_type=jnp.float32)
            best = None if fresh else top[head]
            for chunk in range(tiles * width // HEAD_DIM):
                cut = -(start + chunk * HEAD_DIM)
                piece = part[:, chunk * HEAD_DIM:(chunk + 1) * HEAD_DIM]
                piece = jnp.where((above >= cut) & (below < cut), piece, LEAST)
                scores[turn * per_tile + chunk, head] = piece
                best = piece if best is None else jnp.maximum(best, piece)
            top[head] = best

    per_tile = width // HEAD_DIM
    score(0, common, True)

    @pl.loop(common, count)
    def _(tile):
        score(tile, 1, False)

    for head in range(heads):
        top[head] = jnp.broadcast_to(jnp.max(top[head], axis=1, keepdims=True), top.shape[1:])

    @pl.when(step == 0)
    def _():
        for move in rest:
            move.wait()

    def mix(turn, tiles, fresh):
        start = pl.multiple_of(first + turn * width, GRAIN)
        ones = jnp.ones((tiles * width, HEAD_DIM), vals.dtype)
        for head in range(heads):
            lower = head * HEAD_DIM
            best = top[head]
            weights = jnp.concatenate([
                jnp.exp2((scores[turn * per_tile + chunk, head] - best) * factor).astype(jnp.bfloat16)
                for chunk in range(tiles * per_tile)], axis=1)
            found = jnp.dot(
                weights, jnp.concatenate([vals[pl.ds(start, tiles * width), lower:lower + HEAD_DIM], ones], axis=1),
                preferred_element_type=jnp.float32)
            gathered[head] = found if fresh else gathered[head] + found

    mix(0, common, True)

    @pl.loop(common, count)
    def _(tile):
        mix(tile, 1, False)

    slot = lax.rem(step, 2)

    def leaving(index, place):
        return pltpu.make_async_copy(
            ready.at[place], out_ref.at[pl.ds(pl.multiple_of(index * rows, rows), rows), :], sent.at[place])

    @pl.when(step >= 2)
    def _():
        leaving(step - 2, slot).wait()

    for head in range(heads):
        lower = head * HEAD_DIM
        result = gathered[head]
        ready[slot, :, lower:lower + HEAD_DIM] = (
            result[:, :HEAD_DIM] / result[:, HEAD_DIM:]).astype(ready.dtype)
    leaving(step, slot).start()

    @pl.when(step == steps - 1)
    def _():
        if steps > 1:
            leaving(step - 1, 1 - slot).wait()
        leaving(step, slot).wait()


def distant(array):
    return pltpu.with_memory_space_constraint(array, pltpu.HBM)


def attend(plan, low, span, queries, parts, place, tile_rows, width):
    rows, columns = queries.shape[0], parts[0].shape[1] // 2
    heads = columns // HEAD_DIM
    held = sum(part.shape[0] for part in parts)
    common = -(-(GRAIN + DOC_MOST) // width)
    window = held + max(width, common * width - parts[-1].shape[0])
    most = -(-(GRAIN + DOC_MOST + tile_rows + IMG_LEN) // width)
    near = pl.BlockSpec(memory_space=pltpu.VMEM)
    far = pl.BlockSpec(memory_space=pltpu.HBM)
    return pl.pallas_call(
        functools.partial(attend_kernel, heads=heads, width=width, common=common, place=place),
        out_shape=pltpu.HBM((rows, columns), queries.dtype),
        grid=(rows // tile_rows,),
        in_specs=[far, near, near, far, far, near, far],
        out_specs=far,
        scratch_shapes=[
            pltpu.SMEM(plan.shape, plan.dtype),
            pltpu.VMEM((rows, columns), queries.dtype),
            pltpu.VMEM((window, columns), queries.dtype),
            pltpu.VMEM((window, columns), queries.dtype),
            pltpu.VMEM((most * width // HEAD_DIM, heads, tile_rows, HEAD_DIM), jnp.float32),
            pltpu.VMEM((heads, tile_rows, HEAD_DIM), jnp.float32),
            pltpu.VMEM((heads, tile_rows, 2 * HEAD_DIM), jnp.float32),
            pltpu.VMEM((2, tile_rows, columns), queries.dtype),
            pltpu.SemaphoreType.DMA((2,)),
            pltpu.SemaphoreType.DMA((6,)),
        ],
        compiler_params=pltpu.CompilerParams(
            dimension_semantics=("arbitrary",), vmem_limit_bytes=VMEM_LIMIT),
        cost_estimate=pl.CostEstimate(
            flops=4 * rows * 640 * columns, bytes_accessed=2 * (2 * rows + 2 * held) * columns,
            transcendentals=rows * 640 * heads),
    )(distant(plan), low, span, distant(queries), distant(parts[0]), parts[1], distant(parts[2]))


def spread_kernel(key_ref, value_ref, target_ref, held, came, went):
    parts, rows, columns = held.shape
    piece = columns // (2 * HALVES)

    def coming(part):
        return [
            pltpu.make_async_copy(
                source.at[:, (part * HALVES + half) * piece:(part * HALVES + half + 1) * piece],
                held.at[part, :, (2 * half + side) * piece:(2 * half + side + 1) * piece],
                came.at[part, 2 * half + side])
            for half in range(HALVES) for side, source in enumerate((key_ref, value_ref))
        ]

    def going(part):
        return pltpu.make_async_copy(
            held.at[part], target_ref.at[part * rows:(part + 1) * rows, :], went.at[part])

    for part in range(parts):
        for move in coming(part):
            move.start()
    for part in range(parts):
        for move in coming(part):
            move.wait()
        going(part).start()
    for part in range(parts):
        going(part).wait()


def spread(key_rows, values, parts):
    rows, columns = key_rows.shape
    share = 2 * columns // parts
    return pl.pallas_call(
        spread_kernel,
        out_shape=pltpu.HBM((rows * parts, share), key_rows.dtype),
        in_specs=[pl.BlockSpec(memory_space=pltpu.HBM)] * 2,
        out_specs=pl.BlockSpec(memory_space=pltpu.HBM),
        scratch_shapes=[
            pltpu.VMEM((parts, rows, share), key_rows.dtype),
            pltpu.SemaphoreType.DMA((parts, 2 * HALVES)),
            pltpu.SemaphoreType.DMA((parts,)),
        ],
        compiler_params=pltpu.CompilerParams(vmem_limit_bytes=8 * 2**20),
        cost_estimate=pl.CostEstimate(flops=2**20, bytes_accessed=8 * rows * columns, transcendentals=0),
        name="spread",
    )(distant(key_rows), distant(values))


def weave_kernel(part_ref, *refs, parts, half):
    out_ref, sems = refs[-2:]
    rows, piece = part_ref.shape[0] // parts, part_ref.shape[1]
    moves = [
        pltpu.make_async_copy(
            part_ref.at[part * rows:(part + 1) * rows, :],
            out_ref.at[:, (part * HALVES + half) * piece:(part * HALVES + half + 1) * piece], sems.at[part])
        for part in range(parts)
    ]
    for move in moves:
        move.start()
    for move in moves:
        move.wait()


def weave(array, half, parts, before):
    rows, piece = array.shape
    far = pl.BlockSpec(memory_space=pltpu.HBM)
    return pl.pallas_call(
        functools.partial(weave_kernel, parts=parts, half=half),
        out_shape=pltpu.HBM((rows // parts, piece * parts * HALVES), array.dtype),
        in_specs=[pl.BlockSpec(memory_space=pltpu.VMEM)] + [far] * len(before),
        out_specs=far,
        scratch_shapes=[pltpu.SemaphoreType.DMA((parts,))],
        input_output_aliases={1: 0} if before else {},
        compiler_params=pltpu.CompilerParams(vmem_limit_bytes=8 * 2**20),
        cost_estimate=pl.CostEstimate(flops=2**20, bytes_accessed=4 * rows * piece, transcendentals=0),
    )(array, *before)


def whole_step(queries, key_rows, values, doc_ids, image_flags, labels, token_loss):
    group = ("pair", "head")
    members = lax.axis_size("pair") * lax.axis_size("head")
    local_rows = queries.shape[0]
    rows = local_rows * members
    tile_rows, width = 256, 256

    back = round_up(DOC_MOST - 1, HALO_GRAIN)
    ahead = round_up(IMG_LEN - 1, HALO_GRAIN)
    pairs = lax.all_to_all(spread(key_rows, values, members), group, split_axis=0, concat_axis=0, tiled=True)
    quer = lax.all_to_all(queries, group, split_axis=1, concat_axis=0, tiled=True)
    columns = quer.shape[1]
    halos = []
    for half in range(HALVES):
        lower = half * 2 * columns // HALVES
        upper = lower + 2 * columns // HALVES
        behind = shifted(pairs[rows - back:, lower:upper], "outer", 1)
        front = shifted(pairs[:ahead, lower:upper], "outer", -1)
        halos.append((behind, front))

    documents = doc_ids.shape[0] // DOC_MEAN
    numbers = jnp.arange(documents, dtype=jnp.int32)[:, None]
    places = jnp.arange(doc_ids.shape[0], dtype=jnp.int32)[None, :]
    starts = jnp.sum((doc_ids[None, :] < numbers).astype(jnp.int32), axis=1, keepdims=True)
    image = (doc_ids[None, :] == numbers) & (image_flags[None, :] == 1)
    image_ends = jnp.max(jnp.where(image, places + 1, 0), axis=1, keepdims=True)
    block_start = lax.axis_index("outer") * rows
    block_docs = lax.dynamic_slice_in_dim(doc_ids, block_start, rows)[None, :]
    block_flags = lax.dynamic_slice_in_dim(image_flags, block_start, rows)
    own = block_docs == numbers
    low = jnp.sum(jnp.where(own, starts, 0), axis=0)
    image_high = jnp.sum(jnp.where(own, image_ends, 0), axis=0)
    high = jnp.where(block_flags == 1, image_high, block_start + jnp.arange(rows, dtype=jnp.int32) + 1)
    low = low - (block_start - back)
    high = high - (block_start - back)
    first = low[::tile_rows] // GRAIN * GRAIN
    last = jnp.max(high.reshape(-1, tile_rows), axis=1)
    plan = jnp.stack([first, (last - first + width - 1) // width])

    low, span = low.reshape(-1, HEAD_DIM), (high - low).reshape(-1, HEAD_DIM)
    woven = ()
    for half, (behind, front) in enumerate(halos):
        attended = attend(plan, low, span, quer, (behind, pairs, front), half, tile_rows, width)
        result = lax.all_to_all(attended, group, split_axis=0, concat_axis=0, tiled=True)
        woven = (weave(result, half, members, woven),)
    output, = woven

    row_start = block_start + (lax.axis_index("pair") * lax.axis_size("head") + lax.axis_index("head")) * local_rows
    local_docs = lax.dynamic_slice_in_dim(doc_ids, row_start, local_rows)
    member = (local_docs[:, None] == numbers.T) & (labels[:, None] >= 0)
    counts = jnp.sum(member.astype(jnp.float32), axis=0)
    sums = jnp.sum(jnp.where(member, token_loss[:, None], jnp.float32(0.0)), axis=0)
    totals = jnp.stack([counts, sums])
    for axis in ("outer", "head", "pair"):
        totals = summed(totals, axis)
    counts, sums = totals
    return (output, counts, sums / jnp.maximum(counts, jnp.float32(1.0)))


def solution(mesh):
    blocks, heads = mesh.shape["seq"], mesh.shape["head"]
    pair = 2 if blocks % 2 == 0 else 1
    fine = Mesh(mesh.devices.reshape(blocks // pair, pair, heads), ("outer", "pair", "head"))
    tokens = ("outer", "pair", "head")
    in_specs = (P(tokens, None), P(tokens, None), P(tokens, None), P(), P(), P(tokens), P(tokens))
    out_specs = (P(tokens, None), P(), P())
    return jax.shard_map(whole_step, mesh=fine, in_specs=in_specs, out_specs=out_specs, check_vma=False)
```

time: 158 us -> 140 us (0.89)
  waiting for transfers between devices: 85.2 us -> 69.2 us
  local copies, waits for them, and re-layouts: 14.3 us -> 5.32 us
  Pallas kernels: 19.5 us -> 23.4 us
  starting transfers between devices: 36.1 us -> 38.7 us
    ppermute x5, waiting for transfers between devices: 23.8 us -> 7.95 us  [summed(): lax.ppermute(totals, axis, [(i, i ^ distance) for i in range(size)])]
    all_to_all x4 -> x1, local copies, waits for them, and re-layouts: 8.04 us -> 2.71 us  [whole_step(): lax.all_to_all(queries, group, split_axis=1, concat_axis=0, tiled=True)]
    pallas_call x1 -> x5, Pallas kernels: 19.5 us -> 23.4 us  [the longest x2 17.2 us: attend(): pl.pallas_call(functools.partial(attend_kernel, heads=heads, width=width,...]
    ppermute x4, starting transfers between devices: 10.4 us -> 12.3 us  [shifted(): return lax.ppermute(block, axis, route)]
  transfers between devices with their start and end apart: 13 -> 13, of which waited for: 10 -> 9; matrix products, arithmetic and copies ran while one was open for 7% -> 5% of each run, Pallas kernels for 0% -> 14%
where the time goes in v2:
time: 140 us; the launch traced here: 139 us
  waiting for transfers between devices  69.2 us (49%)
  starting transfers between devices  38.7 us (28%)
  Pallas kernels  23.4 us (17%)
  local copies, waits for them, and re-layouts  5.32 us (4%)
  other arithmetic  1.86 us (1%)
    all_to_all x1, waiting for transfers between devices, whole_step(): lax.all_to_all(spread(key_rows, values, members), group, split_axis=0, co...  35.1 us
    ppermute x4, waiting for transfers between devices, shifted(): return lax.ppermute(block, axis, route)  19.9 us
    pallas_call x2, Pallas kernels, attend(): pl.pallas_call(functools.partial(attend_kernel, heads=heads, width=width,...  17.2 us
    ppermute x4, starting transfers between devices, shifted(): return lax.ppermute(block, axis, route)  12.3 us
    ppermute x5, starting transfers between devices, summed(): lax.ppermute(totals, axis, [(i, i ^ distance) for i in range(size)])  8.59 us
    all_to_all x2, starting transfers between devices, whole_step(): lax.all_to_all(attended, group, split_axis=0, concat_axis=0, tiled=True)  8.12 us
    ppermute x5, waiting for transfers between devices, summed(): lax.ppermute(totals, axis, [(i, i ^ distance) for i in range(size)])  7.95 us
    all_to_all x1, waiting for transfers between devices, whole_step(): lax.all_to_all(queries, group, split_axis=1, concat_axis=0, tiled=True)  6.22 us
  transfers between devices with their start and end apart: 13, of which 9 were waited for; matrix products, arithmetic and copies ran while one was open for 5% of the time, Pallas kernels for 14%

profile of v2, /device:TPU:0, one launch (start us, length us, event | category | flops | bytes accessed | tf_op | source)
XLA Modules:
  0.0 139.3 jit_solution(1557639888340091797)
XLA Ops:
  0.6 3.2 %spread.1 = bf16[1536,1024]{1,0:T(8,128)(2,1)} custom-call(bf16[192,4096]{1,0:T(8,128)(2,1)} %key_ref.1, bf16[192,4096]{1,0:T(8,128)(2,1)} %value_ref.1), custom_call_target="tpu_custom_call" | custom-call | flops 1048576 | bytes 6291456 | tf_op jit(solution)/shard_map/spread/pallas_call | solution.py:245
  3.8 5.2 %all-to-all-start.1 = ((bf16[8,192,1024]{2,1,0:T(8,128)(2,1)}), bf16[8,192,1024]{2,1,0:T(8,128)(2,1)S(1)}, u32[]{:S(2)}, u32[]{:S(2)}) async-start(bf16[8,192,1024]{2,1,0:T(8,128)(2,1)} %bitcast.33), calls=%async_computation.1 | async-start | bytes 6291456 | tf_op jit(solution)/shard_map/all_to_all | solution.py:300
  9.1 2.7 %copy.15 = bf16[24,8,8,512]{3,2,0,1:T(8,128)(2,1)} copy(bf16[24,8,8,512]{3,2,1,0:T(8,128)(2,1)} %bitcast.37) | data formatting | bytes 3145728 | tf_op jit(solution)/shard_map/all_to_all | solution.py:301
  11.8 35.1 %all-to-all-done.1 = bf16[8,192,1024]{2,1,0:T(8,128)(2,1)S(1)} async-done(((bf16[8,192,1024]{2,1,0:T(8,128)(2,1)}), bf16[8,192,1024]{2,1,0:T(8,128)(2,1)S(1)}, u32[]{:S(2)}, u32[]{:S(2)}) %all-to-all-start.1) | async-done | bytes 3145760 | tf_op jit(solution)/shard_map/all_to_all | solution.py:300
  46.9 4.4 %all-to-all-start = ((bf16[192,8,512]{2,0,1:T(8,128)(2,1)}), bf16[192,8,512]{2,0,1:T(8,128)(2,1)}, u32[]{:S(2)}, u32[]{:S(2)}) async-start(bf16[192,8,512]{2,0,1:T(8,128)(2,1)} %bitcast.34), calls=%async_computation | async-start | bytes 3145728 | tf_op jit(solution)/shard_map/all_to_all | solution.py:301
  52.9 4.3 %collective-permute-start.2 = (bf16[704,512]{1,0:T(8,128)(2,1)}, bf16[704,512]{1,0:T(8,128)(2,1)}, u32[]{:S(2)}, u32[]{:S(2)}) collective-permute-start(bf16[704,512]{1,0:T(8,128)(2,1)} %get-tuple-element.18), channel_id=1, source_target_pairs={{0,8},{8,16},{16,24},{1,9},{9,17},{17,25},{2,10},{10,18},{18,26},{... | collective-permute-start | bytes 2162696 | tf_op jit(solution)/shard_map/ppermute | solution.py:29
  60.1 5.4 %collective-permute-start = (bf16[704,512]{1,0:T(8,128)(2,1)}, bf16[704,512]{1,0:T(8,128)(2,1)}, u32[]{:S(2)}, u32[]{:S(2)}) collective-permute-start(bf16[704,512]{1,0:T(8,128)(2,1)} %get-tuple-element.19), channel_id=1, source_target_pairs={{0,8},{8,16},{16,24},{1,9},{9,17},{17,25},{2,10},{10,18},{18,26},{... | collective-permute-start | bytes 2162696 | tf_op jit(solution)/shard_map/ppermute | solution.py:29
  66.1 6.2 %all-to-all-done = bf16[192,8,512]{2,0,1:T(8,128)(2,1)} async-done(((bf16[192,8,512]{2,0,1:T(8,128)(2,1)}), bf16[192,8,512]{2,0,1:T(8,128)(2,1)}, u32[]{:S(2)}, u32[]{:S(2)}) %all-to-all-start) | async-done | bytes 1572896 | tf_op jit(solution)/shard_map/all_to_all | solution.py:301
  72.3 3.6 %collective-permute-done.3.ahead_ref = bf16[576,512]{1,0:T(8,128)(2,1)} collective-permute-done((bf16[576,512]{1,0:T(8,128)(2,1)}, bf16[576,512]{1,0:T(8,128)(2,1)}, u32[]{:S(2)}, u32[]{:S(2)}) %collective-permute-start.3) | collective-permute-done | bytes 589856 | tf_op jit(solution)/shard_map/ppermute | solution.py:29
  75.9 8.6 %shard_map.95 = bf16[1536,256]{1,0:T(8,128)(2,1)} custom-call(s32[2,6]{1,0:T(2,128)} %pad_add_fusion.plan_ref, s32[12,128]{1,0:T(8,128)S(1)} %bitcast.31, s32[12,128]{1,0:T(8,128)S(1)} %get-tuple-element.11.span_ref, bf16[1536,512]{1,0:T(8,128)(2,1)} %bitcast.5.queries_ref, bf16[704,512]{1,0:T(8,128)(2,1)} %collective-permute-done.2.back_ref, ...), custom_call_target="tpu_custom_call" | custom-call | flops 1006632960 | bytes 4456448 | tf_op jit(solution)/shard_map/pallas_call | solution.py:188
  84.6 4.2 %all-to-all-start.3 = ((bf16[8,192,256]{2,1,0:T(8,128)(2,1)}), bf16[8,192,256]{2,1,0:T(8,128)(2,1)}, u32[]{:S(2)}, u32[]{:S(2)}) async-start(bf16[8,192,256]{2,1,0:T(8,128)(2,1)} %bitcast.36), calls=%async_computation.3 | async-start | bytes 1572864 | tf_op jit(solution)/shard_map/all_to_all | solution.py:334
  88.8 1.3 collective-permute-start.1
  90.3 16.3 %collective-permute-done.1.ahead_ref = bf16[576,512]{1,0:T(8,128)(2,1)} collective-permute-done((bf16[576,512]{1,0:T(8,128)(2,1)}, bf16[576,512]{1,0:T(8,128)(2,1)}, u32[]{:S(2)}, u32[]{:S(2)}) %collective-permute-start.1) | collective-permute-done | bytes 589856 | tf_op jit(solution)/shard_map/ppermute | solution.py:29
  106.6 8.6 %shard_map.94 = bf16[1536,256]{1,0:T(8,128)(2,1)} custom-call(s32[2,6]{1,0:T(2,128)} %pad_add_fusion.plan_ref, s32[12,128]{1,0:T(8,128)S(1)} %bitcast.32, s32[12,128]{1,0:T(8,128)S(1)} %get-tuple-element.11.span_ref, bf16[1536,512]{1,0:T(8,128)(2,1)} %bitcast.5.queries_ref, bf16[704,512]{1,0:T(8,128)(2,1)} %collective-permute-done.back_ref, ...), custom_call_target="tpu_custom_call" | custom-call | flops 1006632960 | bytes 4456448 | tf_op jit(solution)/shard_map/pallas_call | solution.py:188
  115.3 3.9 %all-to-all-start.2 = ((bf16[8,192,256]{2,1,0:T(8,128)(2,1)}), bf16[8,192,256]{2,1,0:T(8,128)(2,1)S(1)}, u32[]{:S(2)}, u32[]{:S(2)}) async-start(bf16[8,192,256]{2,1,0:T(8,128)(2,1)} %bitcast.35), calls=%async_computation.2 | async-start | bytes 1572864 | tf_op jit(solution)/shard_map/all_to_all | solution.py:334
  119.2 1.7 %collective-permute-start.4 = (f32[2,16]{1,0:T(2,128)S(1)}, f32[2,16]{1,0:T(2,128)S(1)}, u32[]{:S(2)}, u32[]{:S(2)}) collective-permute-start(f32[2,16]{1,0:T(2,128)S(1)} %pad_maximum_fusion), channel_id=1, source_target_pairs={{0,8},{8,0},{16,24},{24,16},{1,9},{9,1},{17,25},{25,17},{2,10},{10... | collective-permute-start | bytes 392 | tf_op jit(solution)/shard_map/ppermute | solution.py:38
  120.9 1.9 %collective-permute-done.4 = f32[2,16]{1,0:T(2,128)S(1)} collective-permute-done((f32[2,16]{1,0:T(2,128)S(1)}, f32[2,16]{1,0:T(2,128)S(1)}, u32[]{:S(2)}, u32[]{:S(2)}) %collective-permute-start.4) | collective-permute-done | bytes 160 | tf_op jit(solution)/shard_map/ppermute | solution.py:38
  122.8 2.7 %collective-permute-start.5 = (f32[2,16]{1,0:T(2,128)S(1)}, f32[2,16]{1,0:T(2,128)S(1)}, u32[]{:S(2)}, u32[]{:S(2)}) collective-permute-start(f32[2,16]{1,0:T(2,128)S(1)} %fusion.4), channel_id=1, source_target_pairs={{0,16},{8,24},{16,0},{24,8},{1,17},{9,25},{17,1},{25,9},{2,18},{10... | collective-permute-start | bytes 392 | tf_op jit(solution)/shard_map/ppermute | solution.py:38
  125.6 1.8 %collective-permute-done.5 = f32[2,16]{1,0:T(2,128)S(1)} collective-permute-done((f32[2,16]{1,0:T(2,128)S(1)}, f32[2,16]{1,0:T(2,128)S(1)}, u32[]{:S(2)}, u32[]{:S(2)}) %collective-permute-start.5) | collective-permute-done | bytes 160 | tf_op jit(solution)/shard_map/ppermute | solution.py:38
  128.6 2.0 %collective-permute-start.7 = (f32[2,16]{1,0:T(2,128)S(1)}, f32[2,16]{1,0:T(2,128)S(1)}, u32[]{:S(2)}, u32[]{:S(2)}) collective-permute-start(f32[2,16]{1,0:T(2,128)S(1)} %add.62), channel_id=1, source_target_pairs={{0,2},{1,3},{2,0},{3,1},{4,6},{5,7},{6,4},{7,5},{8,10},{9,11},{10,... | collective-permute-start | bytes 392 | tf_op jit(solution)/shard_map/ppermute | solution.py:38
  130.6 1.6 %collective-permute-done.7 = f32[2,16]{1,0:T(2,128)S(1)} collective-permute-done((f32[2,16]{1,0:T(2,128)S(1)}, f32[2,16]{1,0:T(2,128)S(1)}, u32[]{:S(2)}, u32[]{:S(2)}) %collective-permute-start.7) | collective-permute-done | bytes 160 | tf_op jit(solution)/shard_map/ppermute | solution.py:38
  132.2 2.0 %collective-permute-start.8 = (f32[2,16]{1,0:T(2,128)S(1)}, f32[2,16]{1,0:T(2,128)S(1)}, u32[]{:S(2)}, u32[]{:S(2)}) collective-permute-start(f32[2,16]{1,0:T(2,128)S(1)} %add.63), channel_id=1, source_target_pairs={{0,4},{4,0},{1,5},{5,1},{2,6},{6,2},{3,7},{7,3},{8,12},{12,8},{9,1... | collective-permute-start | bytes 392 | tf_op jit(solution)/shard_map/ppermute | solution.py:38
  134.2 1.6 %collective-permute-done.8 = f32[2,16]{1,0:T(2,128)S(1)} collective-permute-done((f32[2,16]{1,0:T(2,128)S(1)}, f32[2,16]{1,0:T(2,128)S(1)}, u32[]{:S(2)}, u32[]{:S(2)}) %collective-permute-start.8) | collective-permute-done | bytes 160 | tf_op jit(solution)/shard_map/ppermute | solution.py:38
  136.3 2.1 %shard_map.96.refs_0_ = bf16[192,4096]{1,0:T(8,128)(2,1)} custom-call(bf16[1536,256]{1,0:T(8,128)(2,1)} %bitcast.12.part_ref), custom_call_target="tpu_custom_call" | custom-call | flops 1048576 | bytes 1572864 | tf_op jit(solution)/shard_map/pallas_call | solution.py:279
  (39 shorter events, 7.9 us)
Async XLA Ops:
  3.8 43.1 %all-to-all-start.1 = ((bf16[8,192,1024]{2,1,0:T(8,128)(2,1)}), bf16[8,192,1024]{2,1,0:T(8,128)(2,1)S(1)}, u32[]{:S(2)}, u32[]{:S(2)}) async-start(bf16[8,192,1024]{2,1,0:T(8,128)(2,1)} %bitcast.33), calls=%async_computation.1 | async-start | bytes 6291456 | tf_op jit(solution)/shard_map/all_to_all | solution.py:300
  9.0 2.7 %copy-start.1 = (s32[6144]{0:T(1024)S(1)}, s32[6144]{0:T(1024)}, u32[]{:S(2)}) copy-start(s32[6144]{0:T(1024)} %param.11) | copy-start | bytes 73732
  46.9 4.5 %copy-start = (s32[6144]{0:T(1024)S(1)}, s32[6144]{0:T(1024)}, u32[]{:S(2)}) copy-start(s32[6144]{0:T(1024)} %param.10) | copy-start | bytes 73732
  46.9 25.4 %all-to-all-start = ((bf16[192,8,512]{2,0,1:T(8,128)(2,1)}), bf16[192,8,512]{2,0,1:T(8,128)(2,1)}, u32[]{:S(2)}, u32[]{:S(2)}) async-start(bf16[192,8,512]{2,0,1:T(8,128)(2,1)} %bitcast.34), calls=%async_computation | async-start | bytes 3145728 | tf_op jit(solution)/shard_map/all_to_all | solution.py:301
  52.9 23.0 %collective-permute-start.2 = (bf16[704,512]{1,0:T(8,128)(2,1)}, bf16[704,512]{1,0:T(8,128)(2,1)}, u32[]{:S(2)}, u32[]{:S(2)}) collective-permute-start(bf16[704,512]{1,0:T(8,128)(2,1)} %get-tuple-element.18), channel_id=1, source_target_pairs={{0,8},{8,16},{16,24},{1,9},{9,17},{17,25},{2,10},{10,18},{18,26},{... | collective-permute-start | bytes 2162696 | tf_op jit(solution)/shard_map/ppermute | solution.py:29
  58.4 17.5 %collective-permute-start.3 = (bf16[576,512]{1,0:T(8,128)(2,1)}, bf16[576,512]{1,0:T(8,128)(2,1)}, u32[]{:S(2)}, u32[]{:S(2)}) collective-permute-start(bf16[576,512]{1,0:T(8,128)(2,1)} %get-tuple-element.16), channel_id=1, source_target_pairs={{8,0},{16,8},{24,16},{9,1},{17,9},{25,17},{10,2},{18,10},{26,18},{... | collective-permute-start | bytes 1769480 | tf_op jit(solution)/shard_map/ppermute | solution.py:29
  60.1 46.5 %collective-permute-start = (bf16[704,512]{1,0:T(8,128)(2,1)}, bf16[704,512]{1,0:T(8,128)(2,1)}, u32[]{:S(2)}, u32[]{:S(2)}) collective-permute-start(bf16[704,512]{1,0:T(8,128)(2,1)} %get-tuple-element.19), channel_id=1, source_target_pairs={{0,8},{8,16},{16,24},{1,9},{9,17},{17,25},{2,10},{10,18},{18,26},{... | collective-permute-start | bytes 2162696 | tf_op jit(solution)/shard_map/ppermute | solution.py:29
  84.6 5.7 %copy-start.3 = (s32[192]{0:T(256)S(1)}, s32[192]{0:T(256)}, u32[]{:S(2)}) copy-start(s32[192]{0:T(256)} %param.12) | copy-start | bytes 2308
  84.6 5.7 %copy-start.2 = (f32[192]{0:T(256)S(1)}, f32[192]{0:T(256)}, u32[]{:S(2)}) copy-start(f32[192]{0:T(256)} %param.13) | copy-start | bytes 2308
  84.6 30.7 %all-to-all-start.3 = ((bf16[8,192,256]{2,1,0:T(8,128)(2,1)}), bf16[8,192,256]{2,1,0:T(8,128)(2,1)}, u32[]{:S(2)}, u32[]{:S(2)}) async-start(bf16[8,192,256]{2,1,0:T(8,128)(2,1)} %bitcast.36), calls=%async_computation.3 | async-start | bytes 1572864 | tf_op jit(solution)/shard_map/all_to_all | solution.py:334
  88.8 17.8 %collective-permute-start.1 = (bf16[576,512]{1,0:T(8,128)(2,1)}, bf16[576,512]{1,0:T(8,128)(2,1)}, u32[]{:S(2)}, u32[]{:S(2)}) collective-permute-start(bf16[576,512]{1,0:T(8,128)(2,1)} %get-tuple-element.17), channel_id=1, source_target_pairs={{8,0},{16,8},{24,16},{9,1},{17,9},{25,17},{10,2},{18,10},{26,18},{... | collective-permute-start | bytes 1769480 | tf_op jit(solution)/shard_map/ppermute | solution.py:29
  115.3 23.1 %all-to-all-start.2 = ((bf16[8,192,256]{2,1,0:T(8,128)(2,1)}), bf16[8,192,256]{2,1,0:T(8,128)(2,1)S(1)}, u32[]{:S(2)}, u32[]{:S(2)}) async-start(bf16[8,192,256]{2,1,0:T(8,128)(2,1)} %bitcast.35), calls=%async_computation.2 | async-start | bytes 1572864 | tf_op jit(solution)/shard_map/all_to_all | solution.py:334
  119.2 3.6 %collective-permute-start.4 = (f32[2,16]{1,0:T(2,128)S(1)}, f32[2,16]{1,0:T(2,128)S(1)}, u32[]{:S(2)}, u32[]{:S(2)}) collective-permute-start(f32[2,16]{1,0:T(2,128)S(1)} %pad_maximum_fusion), channel_id=1, source_target_pairs={{0,8},{8,0},{16,24},{24,16},{1,9},{9,1},{17,25},{25,17},{2,10},{10... | collective-permute-start | bytes 392 | tf_op jit(solution)/shard_map/ppermute | solution.py:38
  122.8 4.5 %collective-permute-start.5 = (f32[2,16]{1,0:T(2,128)S(1)}, f32[2,16]{1,0:T(2,128)S(1)}, u32[]{:S(2)}, u32[]{:S(2)}) collective-permute-start(f32[2,16]{1,0:T(2,128)S(1)} %fusion.4), channel_id=1, source_target_pairs={{0,16},{8,24},{16,0},{24,8},{1,17},{9,25},{17,1},{25,9},{2,18},{10... | collective-permute-start | bytes 392 | tf_op jit(solution)/shard_map/ppermute | solution.py:38
  127.4 1.2 collective-permute-start.6
  128.6 3.6 %collective-permute-start.7 = (f32[2,16]{1,0:T(2,128)S(1)}, f32[2,16]{1,0:T(2,128)S(1)}, u32[]{:S(2)}, u32[]{:S(2)}) collective-permute-start(f32[2,16]{1,0:T(2,128)S(1)} %add.62), channel_id=1, source_target_pairs={{0,2},{1,3},{2,0},{3,1},{4,6},{5,7},{6,4},{7,5},{8,10},{9,11},{10,... | collective-permute-start | bytes 392 | tf_op jit(solution)/shard_map/ppermute | solution.py:38
  132.2 3.6 %collective-permute-start.8 = (f32[2,16]{1,0:T(2,128)S(1)}, f32[2,16]{1,0:T(2,128)S(1)}, u32[]{:S(2)}, u32[]{:S(2)}) collective-permute-start(f32[2,16]{1,0:T(2,128)S(1)} %add.63), channel_id=1, source_target_pairs={{0,4},{4,0},{1,5},{5,1},{2,6},{6,2},{3,7},{7,3},{8,12},{12,8},{9,1... | collective-permute-start | bytes 392 | tf_op jit(solution)/shard_map/ppermute | solution.py:38

commit v3 on v2

--- a/solution.py
+++ b/solution.py
@@ -87,66 +87,81 @@
             lower = (2 * place + side) * columns
             target[back:back + own, :] = own_ref[:, lower:lower + columns]
             target[held:, :] = jnp.zeros((window - held, columns), target.dtype)
-        for move in needs:
+        for move in needs + rest:
             move.wait()
 
-    first = plan[0, step]
-    count = plan[1, step]
-    tile = pl.ds(pl.multiple_of(step * rows, rows), rows)
     lanes = lax.broadcasted_iota(jnp.int32, (rows, HEAD_DIM), 1)
     above = lanes - column(low_ref, step, rows)
     below = above - column(span_ref, step, rows)
 
-    def score(turn, tiles, fresh):
+    per_tile = width // HEAD_DIM
+
+    def score(first, begin, size, turn, tiles, fresh):
         start = pl.multiple_of(first + turn * width, GRAIN)
+        tile = pl.ds(pl.multiple_of(step * rows + begin, size), size)
+        over, under = above[begin:begin + size], below[begin:begin + size]
         for head in range(heads):
             lower = head * HEAD_DIM
             part = lax.dot_general(
                 query[tile, lower:lower + HEAD_DIM], keys[pl.ds(start, tiles * width), lower:lower + HEAD_DIM],
                 (((1,), (1,)), ((), ())), preferred_element_type=jnp.float32)
-            best = None if fresh else top[head]
-            for chunk in range(tiles * width // HEAD_DIM):
+            best = None if fresh else top[head, begin:begin + size]
+            for chunk in range(tiles * per_tile):
                 cut = -(start + chunk * HEAD_DIM)
                 piece = part[:, chunk * HEAD_DIM:(chunk + 1) * HEAD_DIM]
-                piece = jnp.where((above >= cut) & (below < cut), piece, LEAST)
-                scores[turn * per_tile + chunk, head] = piece
+                piece = jnp.where((over >= cut) & (under < cut), piece, LEAST)
+                scores[turn * per_tile + chunk, head, begin:begin + size] = piece
                 best = piece if best is None else jnp.maximum(best, piece)
-            top[head] = best
-
-    per_tile = width // HEAD_DIM
-    score(0, common, True)
-
-    @pl.loop(common, count)
-    def _(tile):
-        score(tile, 1, False)
-
-    for head in range(heads):
-        top[head] = jnp.broadcast_to(jnp.max(top[head], axis=1, keepdims=True), top.shape[1:])
-
-    @pl.when(step == 0)
-    def _():
-        for move in rest:
-            move.wait()
-
-    def mix(turn, tiles, fresh):
+            top[head, begin:begin + size] = best
+
+    def settle(begin, size):
+        for head in range(heads):
+            best = top[head, begin:begin + size]
+            top[head, begin:begin + size] = jnp.broadcast_to(jnp.max(best, axis=1, keepdims=True), best.shape)
+
+    def mix(first, begin, size, turn, tiles, fresh):
         start = pl.multiple_of(first + turn * width, GRAIN)
         ones = jnp.ones((tiles * width, HEAD_DIM), vals.dtype)
         for head in range(heads):
             lower = head * HEAD_DIM
-            best = top[head]
+            best = top[head, begin:begin + size]
             weights = jnp.concatenate([
-                jnp.exp2((scores[turn * per_tile + chunk, head] - best) * factor).astype(jnp.bfloat16)
+                jnp.exp2((scores[turn * per_tile + chunk, head, begin:begin + size] - best) * factor)
+                .astype(jnp.bfloat16)
                 for chunk in range(tiles * per_tile)], axis=1)
             found = jnp.dot(
                 weights, jnp.concatenate([vals[pl.ds(start, tiles * width), lower:lower + HEAD_DIM], ones], axis=1),
                 preferred_element_type=jnp.float32)
-            gathered[head] = found if fresh else gathered[head] + found
-
-    mix(0, common, True)
-
-    @pl.loop(common, count)
-    def _(tile):
-        mix(tile, 1, False)
+            gathered[head, begin:begin + size] = found if fresh else gathered[head, begin:begin + size] + found
+
+    half = rows // 2
+    origin = plan[0, 2 * step]
+    extent = jnp.maximum(plan[1, 2 * step], plan[1, 2 * step + 1]) - origin
+
+    @pl.when(extent <= common * width)
+    def _():
+        score(origin, 0, rows, 0, common, True)
+        settle(0, rows)
+        mix(origin, 0, rows, 0, common, True)
+
+    @pl.when(extent > common * width)
+    def _():
+        for side in range(2):
+            begin = side * half
+            first = plan[0, 2 * step + side]
+            count = (plan[1, 2 * step + side] - first + width - 1) // width
+            score(first, begin, half, 0, common, True)
+
+            @pl.loop(common, count)
+            def _(turn):
+                score(first, begin, half, turn, 1, False)
+
+            settle(begin, half)
+            mix(first, begin, half, 0, common, True)
+
+            @pl.loop(common, count)
+            def _(turn):
+                mix(first, begin, half, turn, 1, False)
 
     slot = lax.rem(step, 2)
 
@@ -288,6 +303,33 @@
     )(array, *before)
 
 
+def cut_kernel(source_ref, tail_ref, head_ref, sems, *, lower):
+    rows, columns = source_ref.shape[0], tail_ref.shape[1]
+    moves = [
+        pltpu.make_async_copy(
+            source_ref.at[start:start + target.shape[0], lower:lower + columns], target, sems.at[index])
+        for index, (start, target) in enumerate(((rows - tail_ref.shape[0], tail_ref), (0, head_ref)))
+    ]
+    for move in moves:
+        move.start()
+    for move in moves:
+        move.wait()
+
+
+def cut(array, back, ahead, half):
+    columns = array.shape[1] // HALVES
+    far = pl.BlockSpec(memory_space=pltpu.HBM)
+    return pl.pallas_call(
+        functools.partial(cut_kernel, lower=half * columns),
+        out_shape=[pltpu.HBM((length, columns), array.dtype) for length in (back, ahead)],
+        in_specs=[pl.BlockSpec(memory_space=pltpu.VMEM)],
+        out_specs=[far, far],
+        scratch_shapes=[pltpu.SemaphoreType.DMA((2,))],
+        compiler_params=pltpu.CompilerParams(vmem_limit_bytes=6 * 2**20),
+        cost_estimate=pl.CostEstimate(flops=2**20, bytes_accessed=4 * (back + ahead) * columns, transcendentals=0),
+    )(array)
+
+
 def whole_step(queries, key_rows, values, doc_ids, image_flags, labels, token_loss):
     group = ("pair", "head")
     members = lax.axis_size("pair") * lax.axis_size("head")
@@ -299,13 +341,11 @@
     ahead = round_up(IMG_LEN - 1, HALO_GRAIN)
     pairs = lax.all_to_all(spread(key_rows, values, members), group, split_axis=0, concat_axis=0, tiled=True)
     quer = lax.all_to_all(queries, group, split_axis=1, concat_axis=0, tiled=True)
-    columns = quer.shape[1]
     halos = []
     for half in range(HALVES):
-        lower = half * 2 * columns // HALVES
-        upper = lower + 2 * columns // HALVES
-        behind = shifted(pairs[rows - back:, lower:upper], "outer", 1)
-        front = shifted(pairs[:ahead, lower:upper], "outer", -1)
+        tail, head = cut(pairs, back, ahead, half)
+        behind = shifted(tail, "outer", 1)
+        front = shifted(head, "outer", -1)
         halos.append((behind, front))
 
     documents = doc_ids.shape[0] // DOC_MEAN
@@ -323,9 +363,8 @@
     high = jnp.where(block_flags == 1, image_high, block_start + jnp.arange(rows, dtype=jnp.int32) + 1)
     low = low - (block_start - back)
     high = high - (block_start - back)
-    first = low[::tile_rows] // GRAIN * GRAIN
-    last = jnp.max(high.reshape(-1, tile_rows), axis=1)
-    plan = jnp.stack([first, (last - first + width - 1) // width])
+    half_rows = tile_rows // 2
+    plan = jnp.stack([low[::half_rows] // GRAIN * GRAIN, jnp.max(high.reshape(-1, half_rows), axis=1)])
 
     low, span = low.reshape(-1, HEAD_DIM), (high - low).reshape(-1, HEAD_DIM)
     woven = ()

time: 140 us -> 140 us (level)
  Pallas kernels: 23.4 us -> 26.2 us
  local copies, waits for them, and re-layouts: 5.32 us -> 2.97 us
    slice x3 -> x1, local copies, waits for them, and re-layouts: 2.43 us -> 0.09 us  [whole_step(): low[::half_rows] // GRAIN * GRAIN]
    pallas_call x0 -> x2, Pallas kernels: none -> 2.18 us  [cut(): pl.pallas_call(functools.partial(cut_kernel, lower=half * columns), out_s...]
  transfers between devices with their start and end apart: 13 -> 13, of which waited for: 9 -> 9; matrix products, arithmetic and copies ran while one was open for 5% -> 4% of each run, Pallas kernels for 14% -> 16%
where the time goes in v3:
time: 140 us; the launch traced here: 139 us
  waiting for transfers between devices  68.7 us (49%)
  starting transfers between devices  38.1 us (27%)
  Pallas kernels  26.2 us (19%)
  local copies, waits for them, and re-layouts  2.97 us (2%)
  other arithmetic  1.98 us (1%)
    all_to_all x1, waiting for transfers between devices, whole_step(): lax.all_to_all(spread(key_rows, values, members), group, split_axis=0, co...  35.1 us
    ppermute x4, waiting for transfers between devices, shifted(): return lax.ppermute(block, axis, route)  18.8 us
    pallas_call x2, Pallas kernels, attend(): pl.pallas_call(functools.partial(attend_kernel, heads=heads, width=width,...  17.9 us
    ppermute x4, starting transfers between devices, shifted(): return lax.ppermute(block, axis, route)  12.4 us
    ppermute x5, waiting for transfers between devices, summed(): lax.ppermute(totals, axis, [(i, i ^ distance) for i in range(size)])  8.56 us
    all_to_all x2, starting transfers between devices, whole_step(): lax.all_to_all(attended, group, split_axis=0, concat_axis=0, tiled=True)  8.09 us
    ppermute x5, starting transfers between devices, summed(): lax.ppermute(totals, axis, [(i, i ^ distance) for i in range(size)])  7.98 us
    all_to_all x1, waiting for transfers between devices, whole_step(): lax.all_to_all(queries, group, split_axis=1, concat_axis=0, tiled=True)  6.21 us
  transfers between devices with their start and end apart: 13, of which 9 were waited for; matrix products, arithmetic and copies ran while one was open for 4% of the time, Pallas kernels for 16%

profile of v3, /device:TPU:0, one launch (start us, length us, event | category | flops | bytes accessed | tf_op | source)
XLA Modules:
  0.0 138.8 jit_solution(7011506852820833718)
XLA Ops:
  0.6 3.2 %spread.1 = bf16[1536,1024]{1,0:T(8,128)(2,1)} custom-call(bf16[192,4096]{1,0:T(8,128)(2,1)} %key_ref.1, bf16[192,4096]{1,0:T(8,128)(2,1)} %value_ref.1), custom_call_target="tpu_custom_call" | custom-call | flops 1048576 | bytes 6291456 | tf_op jit(solution)/shard_map/spread/pallas_call | solution.py:260
  3.8 5.2 %all-to-all-start.1 = ((bf16[8,192,1024]{2,1,0:T(8,128)(2,1)}), bf16[8,192,1024]{2,1,0:T(8,128)(2,1)S(1)}, u32[]{:S(2)}, u32[]{:S(2)}) async-start(bf16[8,192,1024]{2,1,0:T(8,128)(2,1)} %bitcast.35), calls=%async_computation.1 | async-start | bytes 6291456 | tf_op jit(solution)/shard_map/all_to_all | solution.py:342
  9.1 2.7 %copy.15 = bf16[24,8,8,512]{3,2,0,1:T(8,128)(2,1)} copy(bf16[24,8,8,512]{3,2,1,0:T(8,128)(2,1)} %bitcast.39) | data formatting | bytes 3145728 | tf_op jit(solution)/shard_map/all_to_all | solution.py:343
  11.8 35.1 %all-to-all-done.1 = bf16[8,192,1024]{2,1,0:T(8,128)(2,1)S(1)} async-done(((bf16[8,192,1024]{2,1,0:T(8,128)(2,1)}), bf16[8,192,1024]{2,1,0:T(8,128)(2,1)S(1)}, u32[]{:S(2)}, u32[]{:S(2)}) %all-to-all-start.1) | async-done | bytes 3145760 | tf_op jit(solution)/shard_map/all_to_all | solution.py:342
  46.9 4.4 %all-to-all-start = ((bf16[192,8,512]{2,0,1:T(8,128)(2,1)}), bf16[192,8,512]{2,0,1:T(8,128)(2,1)}, u32[]{:S(2)}, u32[]{:S(2)}) async-start(bf16[192,8,512]{2,0,1:T(8,128)(2,1)} %bitcast.36), calls=%async_computation | async-start | bytes 3145728 | tf_op jit(solution)/shard_map/all_to_all | solution.py:343
  52.8 4.4 %collective-permute-start.2 = (bf16[704,512]{1,0:T(8,128)(2,1)}, bf16[704,512]{1,0:T(8,128)(2,1)}, u32[]{:S(2)}, u32[]{:S(2)}) collective-permute-start(bf16[704,512]{1,0:T(8,128)(2,1)} %get-tuple-element.9), channel_id=1, source_target_pairs={{0,8},{8,16},{16,24},{1,9},{9,17},{17,25},{2,10},{10,18},{18,26},{... | collective-permute-start | bytes 2162696 | tf_op jit(solution)/shard_map/ppermute | solution.py:29
  57.3 1.3 collective-permute-start.3
  60.1 5.4 %collective-permute-start = (bf16[704,512]{1,0:T(8,128)(2,1)}, bf16[704,512]{1,0:T(8,128)(2,1)}, u32[]{:S(2)}, u32[]{:S(2)}) collective-permute-start(bf16[704,512]{1,0:T(8,128)(2,1)} %get-tuple-element.7), channel_id=1, source_target_pairs={{0,8},{8,16},{16,24},{1,9},{9,17},{17,25},{2,10},{10,18},{18,26},{... | collective-permute-start | bytes 2162696 | tf_op jit(solution)/shard_map/ppermute | solution.py:29
  66.1 6.2 %all-to-all-done = bf16[192,8,512]{2,0,1:T(8,128)(2,1)} async-done(((bf16[192,8,512]{2,0,1:T(8,128)(2,1)}), bf16[192,8,512]{2,0,1:T(8,128)(2,1)}, u32[]{:S(2)}, u32[]{:S(2)}) %all-to-all-start) | async-done | bytes 1572896 | tf_op jit(solution)/shard_map/all_to_all | solution.py:343
  72.3 2.5 %collective-permute-done.3.ahead_ref = bf16[576,512]{1,0:T(8,128)(2,1)} collective-permute-done((bf16[576,512]{1,0:T(8,128)(2,1)}, bf16[576,512]{1,0:T(8,128)(2,1)}, u32[]{:S(2)}, u32[]{:S(2)}) %collective-permute-start.3) | collective-permute-done | bytes 589856 | tf_op jit(solution)/shard_map/ppermute | solution.py:29
  74.8 8.9 %shard_map.97 = bf16[1536,256]{1,0:T(8,128)(2,1)} custom-call(s32[2,12]{1,0:T(2,128)} %pad_add_fusion.plan_ref, s32[12,128]{1,0:T(8,128)S(1)} %bitcast.33, s32[12,128]{1,0:T(8,128)S(1)} %get-tuple-element.19.span_ref, bf16[1536,512]{1,0:T(8,128)(2,1)} %bitcast.6.queries_ref, bf16[704,512]{1,0:T(8,128)(2,1)} %collective-permute-done.2.back_ref, ...), custom_call_target="tpu_custom_call" | custom-call | flops 1006632960 | bytes 4456448 | tf_op jit(solution)/shard_map/pallas_call | solution.py:203
  83.8 4.2 %all-to-all-start.3 = ((bf16[8,192,256]{2,1,0:T(8,128)(2,1)}), bf16[8,192,256]{2,1,0:T(8,128)(2,1)}, u32[]{:S(2)}, u32[]{:S(2)}) async-start(bf16[8,192,256]{2,1,0:T(8,128)(2,1)} %bitcast.38), calls=%async_computation.3 | async-start | bytes 1572864 | tf_op jit(solution)/shard_map/all_to_all | solution.py:373
  88.0 1.3 collective-permute-start.1
  89.6 16.3 %collective-permute-done.1.ahead_ref = bf16[576,512]{1,0:T(8,128)(2,1)} collective-permute-done((bf16[576,512]{1,0:T(8,128)(2,1)}, bf16[576,512]{1,0:T(8,128)(2,1)}, u32[]{:S(2)}, u32[]{:S(2)}) %collective-permute-start.1) | collective-permute-done | bytes 589856 | tf_op jit(solution)/shard_map/ppermute | solution.py:29
  105.9 8.9 %shard_map.95 = bf16[1536,256]{1,0:T(8,128)(2,1)} custom-call(s32[2,12]{1,0:T(2,128)} %pad_add_fusion.plan_ref, s32[12,128]{1,0:T(8,128)S(1)} %bitcast.34, s32[12,128]{1,0:T(8,128)S(1)} %get-tuple-element.19.span_ref, bf16[1536,512]{1,0:T(8,128)(2,1)} %bitcast.6.queries_ref, bf16[704,512]{1,0:T(8,128)(2,1)} %collective-permute-done.back_ref, ...), custom_call_target="tpu_custom_call" | custom-call | flops 1006632960 | bytes 4456448 | tf_op jit(solution)/shard_map/pallas_call | solution.py:203
  114.8 3.9 %all-to-all-start.2 = ((bf16[8,192,256]{2,1,0:T(8,128)(2,1)}), bf16[8,192,256]{2,1,0:T(8,128)(2,1)S(1)}, u32[]{:S(2)}, u32[]{:S(2)}) async-start(bf16[8,192,256]{2,1,0:T(8,128)(2,1)} %bitcast.37), calls=%async_computation.2 | async-start | bytes 1572864 | tf_op jit(solution)/shard_map/all_to_all | solution.py:373
  119.8 2.5 %collective-permute-done.4 = f32[2,16]{1,0:T(2,128)S(1)} collective-permute-done((f32[2,16]{1,0:T(2,128)S(1)}, f32[2,16]{1,0:T(2,128)S(1)}, u32[]{:S(2)}, u32[]{:S(2)}) %collective-permute-start.4) | collective-permute-done | bytes 160 | tf_op jit(solution)/shard_map/ppermute | solution.py:38
  122.3 2.7 %collective-permute-start.5 = (f32[2,16]{1,0:T(2,128)S(1)}, f32[2,16]{1,0:T(2,128)S(1)}, u32[]{:S(2)}, u32[]{:S(2)}) collective-permute-start(f32[2,16]{1,0:T(2,128)S(1)} %fusion.2), channel_id=1, source_target_pairs={{0,16},{8,24},{16,0},{24,8},{1,17},{9,25},{17,1},{25,9},{2,18},{10... | collective-permute-start | bytes 392 | tf_op jit(solution)/shard_map/ppermute | solution.py:38
  125.0 1.8 %collective-permute-done.5 = f32[2,16]{1,0:T(2,128)S(1)} collective-permute-done((f32[2,16]{1,0:T(2,128)S(1)}, f32[2,16]{1,0:T(2,128)S(1)}, u32[]{:S(2)}, u32[]{:S(2)}) %collective-permute-start.5) | collective-permute-done | bytes 160 | tf_op jit(solution)/shard_map/ppermute | solution.py:38
  128.1 2.0 %collective-permute-start.7 = (f32[2,16]{1,0:T(2,128)S(1)}, f32[2,16]{1,0:T(2,128)S(1)}, u32[]{:S(2)}, u32[]{:S(2)}) collective-permute-start(f32[2,16]{1,0:T(2,128)S(1)} %add.57), channel_id=1, source_target_pairs={{0,2},{1,3},{2,0},{3,1},{4,6},{5,7},{6,4},{7,5},{8,10},{9,11},{10,... | collective-permute-start | bytes 392 | tf_op jit(solution)/shard_map/ppermute | solution.py:38
  130.1 1.6 %collective-permute-done.7 = f32[2,16]{1,0:T(2,128)S(1)} collective-permute-done((f32[2,16]{1,0:T(2,128)S(1)}, f32[2,16]{1,0:T(2,128)S(1)}, u32[]{:S(2)}, u32[]{:S(2)}) %collective-permute-start.7) | collective-permute-done | bytes 160 | tf_op jit(solution)/shard_map/ppermute | solution.py:38
  131.7 2.0 %collective-permute-start.8 = (f32[2,16]{1,0:T(2,128)S(1)}, f32[2,16]{1,0:T(2,128)S(1)}, u32[]{:S(2)}, u32[]{:S(2)}) collective-permute-start(f32[2,16]{1,0:T(2,128)S(1)} %add.58), channel_id=1, source_target_pairs={{0,4},{4,0},{1,5},{5,1},{2,6},{6,2},{3,7},{7,3},{8,12},{12,8},{9,1... | collective-permute-start | bytes 392 | tf_op jit(solution)/shard_map/ppermute | solution.py:38
  133.7 1.6 %collective-permute-done.8 = f32[2,16]{1,0:T(2,128)S(1)} collective-permute-done((f32[2,16]{1,0:T(2,128)S(1)}, f32[2,16]{1,0:T(2,128)S(1)}, u32[]{:S(2)}, u32[]{:S(2)}) %collective-permute-start.8) | collective-permute-done | bytes 160 | tf_op jit(solution)/shard_map/ppermute | solution.py:38
  135.8 2.1 %shard_map.98.refs_0_ = bf16[192,4096]{1,0:T(8,128)(2,1)} custom-call(bf16[1536,256]{1,0:T(8,128)(2,1)} %bitcast.13.part_ref), custom_call_target="tpu_custom_call" | custom-call | flops 1048576 | bytes 1572864 | tf_op jit(solution)/shard_map/pallas_call | solution.py:294
  (38 shorter events, 7.8 us)
Async XLA Ops:
  3.8 43.1 %all-to-all-start.1 = ((bf16[8,192,1024]{2,1,0:T(8,128)(2,1)}), bf16[8,192,1024]{2,1,0:T(8,128)(2,1)S(1)}, u32[]{:S(2)}, u32[]{:S(2)}) async-start(bf16[8,192,1024]{2,1,0:T(8,128)(2,1)} %bitcast.35), calls=%async_computation.1 | async-start | bytes 6291456 | tf_op jit(solution)/shard_map/all_to_all | solution.py:342
  46.9 4.4 %copy-start.1 = (s32[6144]{0:T(1024)S(1)}, s32[6144]{0:T(1024)}, u32[]{:S(2)}) copy-start(s32[6144]{0:T(1024)} %param.10) | copy-start | bytes 73732
  46.9 4.5 %copy-start = (s32[6144]{0:T(1024)S(1)}, s32[6144]{0:T(1024)}, u32[]{:S(2)}) copy-start(s32[6144]{0:T(1024)} %param.11) | copy-start | bytes 73732
  46.9 25.4 %all-to-all-start = ((bf16[192,8,512]{2,0,1:T(8,128)(2,1)}), bf16[192,8,512]{2,0,1:T(8,128)(2,1)}, u32[]{:S(2)}, u32[]{:S(2)}) async-start(bf16[192,8,512]{2,0,1:T(8,128)(2,1)} %bitcast.36), calls=%async_computation | async-start | bytes 3145728 | tf_op jit(solution)/shard_map/all_to_all | solution.py:343
  52.8 22.0 %collective-permute-start.2 = (bf16[704,512]{1,0:T(8,128)(2,1)}, bf16[704,512]{1,0:T(8,128)(2,1)}, u32[]{:S(2)}, u32[]{:S(2)}) collective-permute-start(bf16[704,512]{1,0:T(8,128)(2,1)} %get-tuple-element.9), channel_id=1, source_target_pairs={{0,8},{8,16},{16,24},{1,9},{9,17},{17,25},{2,10},{10,18},{18,26},{... | collective-permute-start | bytes 2162696 | tf_op jit(solution)/shard_map/ppermute | solution.py:29
  57.3 17.5 %collective-permute-start.3 = (bf16[576,512]{1,0:T(8,128)(2,1)}, bf16[576,512]{1,0:T(8,128)(2,1)}, u32[]{:S(2)}, u32[]{:S(2)}) collective-permute-start(bf16[576,512]{1,0:T(8,128)(2,1)} %get-tuple-element.10), channel_id=1, source_target_pairs={{8,0},{16,8},{24,16},{9,1},{17,9},{25,17},{10,2},{18,10},{26,18},{... | collective-permute-start | bytes 1769480 | tf_op jit(solution)/shard_map/ppermute | solution.py:29
  60.1 45.8 %collective-permute-start = (bf16[704,512]{1,0:T(8,128)(2,1)}, bf16[704,512]{1,0:T(8,128)(2,1)}, u32[]{:S(2)}, u32[]{:S(2)}) collective-permute-start(bf16[704,512]{1,0:T(8,128)(2,1)} %get-tuple-element.7), channel_id=1, source_target_pairs={{0,8},{8,16},{16,24},{1,9},{9,17},{17,25},{2,10},{10,18},{18,26},{... | collective-permute-start | bytes 2162696 | tf_op jit(solution)/shard_map/ppermute | solution.py:29
  83.8 5.7 %copy-start.3 = (s32[192]{0:T(256)S(1)}, s32[192]{0:T(256)}, u32[]{:S(2)}) copy-start(s32[192]{0:T(256)} %param.12) | copy-start | bytes 2308
  83.8 5.6 %copy-start.2 = (f32[192]{0:T(256)S(1)}, f32[192]{0:T(256)}, u32[]{:S(2)}) copy-start(f32[192]{0:T(256)} %param.13) | copy-start | bytes 2308
  83.8 31.0 %all-to-all-start.3 = ((bf16[8,192,256]{2,1,0:T(8,128)(2,1)}), bf16[8,192,256]{2,1,0:T(8,128)(2,1)}, u32[]{:S(2)}, u32[]{:S(2)}) async-start(bf16[8,192,256]{2,1,0:T(8,128)(2,1)} %bitcast.38), calls=%async_computation.3 | async-start | bytes 1572864 | tf_op jit(solution)/shard_map/all_to_all | solution.py:373
  88.0 17.8 %collective-permute-start.1 = (bf16[576,512]{1,0:T(8,128)(2,1)}, bf16[576,512]{1,0:T(8,128)(2,1)}, u32[]{:S(2)}, u32[]{:S(2)}) collective-permute-start(bf16[576,512]{1,0:T(8,128)(2,1)} %get-tuple-element.8), channel_id=1, source_target_pairs={{8,0},{16,8},{24,16},{9,1},{17,9},{25,17},{10,2},{18,10},{26,18},{... | collective-permute-start | bytes 1769480 | tf_op jit(solution)/shard_map/ppermute | solution.py:29
  114.8 23.1 %all-to-all-start.2 = ((bf16[8,192,256]{2,1,0:T(8,128)(2,1)}), bf16[8,192,256]{2,1,0:T(8,128)(2,1)S(1)}, u32[]{:S(2)}, u32[]{:S(2)}) async-start(bf16[8,192,256]{2,1,0:T(8,128)(2,1)} %bitcast.37), calls=%async_computation.2 | async-start | bytes 1572864 | tf_op jit(solution)/shard_map/all_to_all | solution.py:373
  118.7 3.6 %collective-permute-start.4 = (f32[2,16]{1,0:T(2,128)S(1)}, f32[2,16]{1,0:T(2,128)S(1)}, u32[]{:S(2)}, u32[]{:S(2)}) collective-permute-start(f32[2,16]{1,0:T(2,128)S(1)} %pad_maximum_fusion), channel_id=1, source_target_pairs={{0,8},{8,0},{16,24},{24,16},{1,9},{9,1},{17,25},{25,17},{2,10},{10... | collective-permute-start | bytes 392 | tf_op jit(solution)/shard_map/ppermute | solution.py:38
  122.3 4.5 %collective-permute-start.5 = (f32[2,16]{1,0:T(2,128)S(1)}, f32[2,16]{1,0:T(2,128)S(1)}, u32[]{:S(2)}, u32[]{:S(2)}) collective-permute-start(f32[2,16]{1,0:T(2,128)S(1)} %fusion.2), channel_id=1, source_target_pairs={{0,16},{8,24},{16,0},{24,8},{1,17},{9,25},{17,1},{25,9},{2,18},{10... | collective-permute-start | bytes 392 | tf_op jit(solution)/shard_map/ppermute | solution.py:38
  126.9 1.2 collective-permute-start.6
  128.1 3.6 %collective-permute-start.7 = (f32[2,16]{1,0:T(2,128)S(1)}, f32[2,16]{1,0:T(2,128)S(1)}, u32[]{:S(2)}, u32[]{:S(2)}) collective-permute-start(f32[2,16]{1,0:T(2,128)S(1)} %add.57), channel_id=1, source_target_pairs={{0,2},{1,3},{2,0},{3,1},{4,6},{5,7},{6,4},{7,5},{8,10},{9,11},{10,... | collective-permute-start | bytes 392 | tf_op jit(solution)/shard_map/ppermute | solution.py:38
  131.7 3.6 %collective-permute-start.8 = (f32[2,16]{1,0:T(2,128)S(1)}, f32[2,16]{1,0:T(2,128)S(1)}, u32[]{:S(2)}, u32[]{:S(2)}) collective-permute-start(f32[2,16]{1,0:T(2,128)S(1)} %add.58), channel_id=1, source_target_pairs={{0,4},{4,0},{1,5},{5,1},{2,6},{6,2},{3,7},{7,3},{8,12},{12,8},{9,1... | collective-permute-start | bytes 392 | tf_op jit(solution)/shard_map/ppermute | solution.py:38
